TPU v7x, 32 devices: a 4x2x2 block of a 4x4x8 slice. The times are simulated.
32 devices in a mesh: dp: 4 (over y, z), ep: 8 (over x, core).
Axes of the slice: x: 4, y: 2, z: 2, core: 2. Of those that a mesh axis runs over, the one named last changes fastest.
The devices are a block of a 4x4x8 slice.
Arguments:
- hidden: bfloat16 [3072, 2048], P(('dp', 'ep')), parts along dimension 0
- norm_gain: bfloat16 [2048], replicated
- w_gate: bfloat16 [2048, 64], replicated
- w1_shared: bfloat16 [2048, 2816], replicated
- w3_shared: bfloat16 [2048, 2816], replicated
- w2_shared: bfloat16 [2816, 2048], replicated
- w1_experts: bfloat16 [64, 2048, 1408], P('ep')
- w3_experts: bfloat16 [64, 2048, 1408], P('ep')
- w2_experts: bfloat16 [64, 1408, 2048], P('ep')
- topk_ids: int32 [3072, 6], P(('dp', 'ep')), parts along dimension 0
Outputs:
- output: bfloat16 [3072, 2048], P(('dp', 'ep')), parts along dimension 0
There are 4 independent parts. A program takes and returns all parts, laid end to end along the dimension named above; an argument that names none is the same for every part.
All inputs are finite; a program needn't handle non-finite values.
Results may differ from a plain program's by a relative error of at most 0.00585255.
Values are sent between devices in bfloat16 or wider.
A program may use at most 768 MiB of HBM per device.

v0:
```python
import jax
import jax.numpy as jnp
from jax import lax
from jax.sharding import PartitionSpec as P

ROUTE_SCALE = 16
NORM_EPS = 1e-6


def rms_norm(hidden, norm_gain):
    rows_f = hidden.astype(jnp.float32)
    inv_rms = lax.rsqrt(jnp.mean(rows_f * rows_f, axis=-1, keepdims=True) + NORM_EPS)
    return (rows_f * inv_rms * norm_gain.astype(jnp.float32)).astype(jnp.bfloat16)


def swiglu(rows_in, w_up, w_lin, w_down):
    gate_act = jnp.dot(rows_in, w_up, preferred_element_type=jnp.float32)
    lin_act = jnp.dot(rows_in, w_lin, preferred_element_type=jnp.float32)
    inner_act = (jax.nn.silu(gate_act) * lin_act).astype(jnp.bfloat16)
    return jnp.dot(inner_act, w_down, preferred_element_type=jnp.float32).astype(jnp.bfloat16)


def router_weights(normed, w_gate, topk_ids):
    gate_probs = jax.nn.softmax(jnp.dot(normed, w_gate, preferred_element_type=jnp.float32), axis=-1)
    return ROUTE_SCALE * jnp.take_along_axis(gate_probs, topk_ids, axis=1)


def routed_experts(rows_in, row_wts, w1_experts, w3_experts, w2_experts):
    gate_act = jnp.einsum('nd,edf->enf', rows_in, w1_experts, preferred_element_type=jnp.float32)
    lin_act = jnp.einsum('nd,edf->enf', rows_in, w3_experts, preferred_element_type=jnp.float32)
    inner_act = (jax.nn.silu(gate_act) * lin_act).astype(jnp.bfloat16)
    expert_out = jnp.einsum('enf,efd->end', inner_act, w2_experts, preferred_element_type=jnp.float32).astype(jnp.bfloat16)
    return jnp.sum(expert_out * row_wts.T[:, :, None], axis=0)


def solution(mesh):
    tok_spec = P(('dp', 'ep'), None)
    expert_spec = P('ep', None, None)

    def local_fn(hidden, norm_gain, w_gate, w1_shared, w3_shared, w2_shared, w1_experts, w3_experts, w2_experts, topk_ids):
        normed = rms_norm(hidden, norm_gain)
        gate_wts = router_weights(normed, w_gate, topk_ids)
        shared_out = swiglu(normed, w1_shared, w3_shared, w2_shared)
        all_rows = lax.all_gather(normed, 'ep', axis=0, tiled=True)
        all_ids = lax.all_gather(topk_ids, 'ep', axis=0, tiled=True)
        all_wts = lax.all_gather(gate_wts, 'ep', axis=0, tiled=True)
        local_count = w1_experts.shape[0]
        local_ids = lax.axis_index('ep') * local_count + jnp.arange(local_count)
        row_wts = jnp.sum(jnp.where(all_ids[:, :, None] == local_ids, all_wts[:, :, None], 0.0), axis=1)
        part_sum = routed_experts(all_rows, row_wts, w1_experts, w3_experts, w2_experts)
        routed = lax.psum_scatter(part_sum, 'ep', scatter_dimension=0, tiled=True)
        return (hidden.astype(jnp.float32) + shared_out.astype(jnp.float32) + routed).astype(jnp.bfloat16)

    return jax.shard_map(local_fn, mesh=mesh, in_specs=(tok_spec, P(), P(), P(), P(), P(), expert_spec, expert_spec, expert_spec, tok_spec), out_specs=tok_spec, check_vma=False)
```

profile of v0, /device:TPU:81, one launch (start us, length us, event | category | flops | bytes accessed | tf_op | source)
XLA Modules:
  0.0 256.7 jit_solution(10825556094615033785)
XLA Ops:
  6.5 0.0 copy-start
  6.6 0.0 all-gather.4.cloned.1.call-start
  6.6 0.7 convert_element_type.32
  7.3 1.2 fusion.12
  8.5 0.0 copy-start.7
  8.5 1.9 fusion.14
  10.4 0.1 all-gather.4.cloned.1.call-update
  10.5 0.1 reduce-scatter.2.cloned.1.call-start
  10.5 0.7 bitcast_or_fusion
  11.2 0.1 copy.39
  11.3 0.1 reshape.28
  11.5 0.0 copy-done
  11.5 1.3 fusion.25
  12.9 0.0 copy-start.5
  12.9 4.0 %gather_fusion = f32[576]{0:T(1024)S(1)} fusion(f32[96,64]{0,1:T(8,128)S(1)} %fusion.16, s32[576]{0:T(1024)S(1)} %reshape.28), kind=kCustom, calls=%fused_computation | custom fusion | bytes 9216 | tf_op jit(solution)/shard_map/jit(take_along_axis)/gather | solution.py:25
  17.0 0.0 copy-done.3
  17.0 0.0 copy-done.7
  17.0 0.1 reshape.31
  17.1 0.1 copy.40
  17.2 14.9 %all-gather.1 = f32[8,96,6]{1,2,0:T(8,128)S(1)} all-gather(f32[1,96,6]{1,2,0:T(8,128)S(1)} %multiply_bitcast_fusion), channel_id=1, replica_groups=mesh['dp'=4,'ep'=8] {'ep'}, dimensions={0}, use_global_device_ids=true | all-gather | bytes 20736 | tf_op jit(solution)/shard_map/all_gather | solution.py:46
  32.1 0.1 reshape.42
  32.2 13.1 %all-gather = s32[8,96,6]{1,2,0:T(8,128)S(1)} all-gather(s32[1,96,6]{1,2,0:T(8,128)S(1)} %bitcast.75), channel_id=1, replica_groups=mesh['dp'=4,'ep'=8] {'ep'}, dimensions={0}, use_global_device_ids=true | all-gather | bytes 20736 | tf_op jit(solution)/shard_map/all_gather | solution.py:45
  45.3 0.1 reshape.40
  45.4 0.7 select_reduce_fusion
  46.1 47.9 %fusion.5 = f32[768,8,1408]{2,0,1:T(8,128)} fusion(bf16[8,2048,1408]{2,1,0:T(8,128)(2,1)} %param.17, bf16[768,2048]{1,0:T(8,128)(2,1)} %all-gather.4.cloned.1.call-done), kind=kOutput, calls=%fused_computation.11 | convolution fusion | flops 35433480192 | bytes 83886080 | tf_op jit(solution)/shard_map/nd,edf->enf/dot_general | solution.py:30
  94.0 52.7 %fusion.51 = bf16[8,768,1408]{2,1,0:T(8,128)(2,1)} fusion(f32[768,8,1408]{2,0,1:T(8,128)} %fusion.5, bf16[8,2048,1408]{2,1,0:T(8,128)(2,1)} %param.16, bf16[768,2048]{1,0:T(8,128)(2,1)S(1)} %copy-done.9), kind=kOutput, calls=%bitcast_fusion.clone.1 | convolution fusion | flops 35485384704 | bytes 101187584 | tf_op jit(solution)/shard_map/nd,edf->enf/dot_general | solution.py:29
  146.7 49.4 %multiply_reduce_fusion = f32[768,2048]{1,0:T(8,128)} fusion(f32[8,768]{1,0:T(8,128)S(1)} %bitcast.76, bf16[8,1408,2048]{2,1,0:T(8,128)(2,1)} %param.18, bf16[8,768,1408]{2,1,0:T(8,128)(2,1)} %fusion.51), kind=kOutput, calls=%fused_computation.1 | convolution fusion | flops 35482238976 | bytes 69754880 | tf_op jit(solution)/shard_map/enf,efd->end/dot_general | solution.py:32
  196.1 0.1 reduce-scatter.2.cloned.1.call-update
  196.2 0.0 copy-start.1
  196.2 6.3 %fusion.23 = f32[96,2816]{1,0:T(8,128)S(1)} fusion(bf16[2048,2816]{1,0:T(8,128)(2,1)} %param.13, bf16[96,2048]{1,0:T(8,128)(2,1)S(1)} %copy-done.2, f32[2048]{0:T(1024)S(1)} %copy-done.4, f32[96]{0:T(128)S(1)} %copy-done.8), kind=kOutput, calls=%fused_computation.36 | convolution fusion | flops 1108082688 | bytes 13017472 | tf_op jit(solution)/shard_map/dot_general | solution.py:17
  202.5 34.8 %reduce-scatter.2.cloned.1.call-done = f32[96,2048]{1,0:T(8,128)} async-done(((f32[768,2048]{1,0:T(8,128)}), f32[96,2048]{1,0:T(8,128)}) %reduce-scatter.2.cloned.1.call-update) | async-done | bytes 786448 | tf_op jit(solution)/shard_map/reduce_scatter | solution.py:51
  237.4 12.4 %fusion.11 = bf16[96,2048]{1,0:T(8,128)(2,1)} fusion(f32[96,2048]{1,0:T(8,128)} %reduce-scatter.2.cloned.1.call-done, bf16[2816,2048]{1,0:T(8,128)(2,1)} %param.15, bf16[96,2048]{1,0:T(8,128)(2,1)S(1)} %copy-done.2, bf16[2048,2816]{1,0:T(8,128)(2,1)} %param.14, f32[96,2816]{1,0:T(8,128)S(1)} %fusion.23, f32[2048]{0:T(1024)S(1)} %copy-done.4, ...), kind=kOutput, calls=%fused_computation.18 | convolution fusion | flops 2218180608 | bytes 25731456 | tf_op jit(solution)/shard_map/dot_general | solution.py:20
  (21 shorter events, 0.1 us)
Async XLA Ops:
  6.5 4.9 %copy-start = (bf16[2048,64]{0,1:T(8,128)(2,1)S(1)}, bf16[2048,64]{0,1:T(8,128)(2,1)}, u32[]{:S(2)}) copy-start(bf16[2048,64]{0,1:T(8,128)(2,1)} %param.12) | copy-start | bytes 786436
  6.6 39.5 %all-gather.4.cloned.1.call-start = ((), (), s32[]{:S(2)}) async-start(), calls=%async_computation.1 | async-start | bytes 3538944 | tf_op jit(solution)/shard_map/all_gather | solution.py:44
  7.3 9.7 %copy-start.3 = (f32[2048]{0:T(1024)}, f32[2048]{0:T(1024)S(1)}, u32[]{:S(2)}) copy-start(f32[2048]{0:T(1024)S(1)} %convert_element_type.32) | copy-start | bytes 24580
  8.5 8.5 %copy-start.7 = (f32[96]{0:T(128)}, f32[96]{0:T(128)S(1)}, u32[]{:S(2)}) copy-start(f32[96]{0:T(128)S(1)} %add_rsqrt_fusion) | copy-start | bytes 1156
  10.5 226.9 %reduce-scatter.2.cloned.1.call-start = ((), (), s32[]{:S(2)}) async-start(), calls=%async_computation.2 | async-start | bytes 7077888 | tf_op jit(solution)/shard_map/reduce_scatter | solution.py:51
  12.9 4.3 %copy-start.5 = (s32[96,6]{0,1:T(8,128)S(1)}, s32[96,6]{0,1:T(8,128)}, u32[]{:S(2)}) copy-start(s32[96,6]{0,1:T(8,128)} %param.19) | copy-start | bytes 6916
  46.1 47.9 %copy-start.9 = (bf16[768,2048]{1,0:T(8,128)(2,1)S(1)}, bf16[768,2048]{1,0:T(8,128)(2,1)}, u32[]{:S(2)}) copy-start(bf16[768,2048]{1,0:T(8,128)(2,1)} %all-gather.4.cloned.1.call-done) | copy-start | bytes 9437188
  94.0 52.7 %copy-start.6 = (f32[768,8]{0,1:T(8,128)S(1)}, f32[768,8]{0,1:T(8,128)}, u32[]{:S(2)}) copy-start(f32[768,8]{0,1:T(8,128)} %select_reduce_fusion) | copy-start | bytes 73732
  146.7 49.5 %copy-start.2 = (bf16[96,2048]{1,0:T(8,128)(2,1)S(1)}, bf16[96,2048]{1,0:T(8,128)(2,1)}, u32[]{:S(2)}) copy-start(bf16[96,2048]{1,0:T(8,128)(2,1)} %param.10) | copy-start | bytes 1179652
  146.7 49.5 %copy-start.4 = (f32[2048]{0:T(1024)S(1)}, f32[2048]{0:T(1024)}, u32[]{:S(2)}) copy-start(f32[2048]{0:T(1024)} %copy-done.3) | copy-start | bytes 24580
  146.7 49.5 %copy-start.8 = (f32[96]{0:T(128)S(1)}, f32[96]{0:T(128)}, u32[]{:S(2)}) copy-start(f32[96]{0:T(128)} %copy-done.7) | copy-start | bytes 1156
  196.2 53.6 %copy-start.1 = (bf16[2048,64]{0,1:T(8,128)(2,1)S(1)}, bf16[2048,64]{0,1:T(8,128)(2,1)}, u32[]{:S(2)}) copy-start(bf16[2048,64]{0,1:T(8,128)(2,1)} %param.12) | copy-start | bytes 786436
Sparse Core Ops, SparseCore 0:
  10.6 29.2 all-gather.3
  196.3 41.0 reduce-scatter.1
where the time goes:
time: 257 us
  matrix products  170 us (66%)
  waiting for transfers between devices  34.9 us (14%)
  blocking collectives  28 us (11%)
  between operations  13.6 us (5%)
  other arithmetic  5.27 us (2%)
  local copies, waits for them, and re-layouts  4.69 us (2%)
    dot_general x1, matrix products, routed_experts(): jnp.einsum('nd,edf->enf', rows_in, w1_experts, preferred_element_type=jnp...  52.7 us
    dot_general x1, matrix products, routed_experts(): jnp.einsum('enf,efd->end', inner_act, w2_experts, preferred_element_type=...  49.4 us
    dot_general x1, matrix products, routed_experts(): jnp.einsum('nd,edf->enf', rows_in, w3_experts, preferred_element_type=jnp...  47.9 us
    reduce_scatter x1, waiting for transfers between devices, local_fn(): routed = lax.psum_scatter(part_sum, 'ep', scatter_dimension=0, tiled=True)  34.8 us
    all_gather x1, blocking collectives, local_fn(): all_wts = lax.all_gather(gate_wts, 'ep', axis=0, tiled=True)  14.9 us
    all_gather x1, blocking collectives, local_fn(): all_ids = lax.all_gather(topk_ids, 'ep', axis=0, tiled=True)  13.1 us
    dot_general x1, matrix products, swiglu(): jnp.dot(inner_act, w_down, preferred_element_type=jnp.float32)  12.4 us
    dot_general x1, matrix products, swiglu(): gate_act = jnp.dot(rows_in, w_up, preferred_element_type=jnp.float32)  6.35 us
  transfers between devices with their start and end apart: 2, of which 1 were waited for; matrix products, arithmetic and copies ran while one was open for 5% of the time, Pallas kernels for 0%

commit v1 on v0

v1 whole, which is shorter than its diff:
```python
import functools

import jax
import jax.numpy as jnp
from jax import lax
from jax.experimental import pallas as pl
from jax.experimental.pallas import tpu as pltpu
from jax.sharding import PartitionSpec as P

ROUTE_SCALE = 16
NORM_EPS = 1e-6
CAP = 128
K_CHUNKS = 4
J_CHUNKS = 8
UP_SLOTS = 5
DOWN_SLOTS = 8
LAG = 2

F32 = jnp.float32
BF16 = jnp.bfloat16


def rms_norm(hidden, norm_gain):
    rows_f = hidden.astype(F32)
    inv_rms = lax.rsqrt(jnp.mean(rows_f * rows_f, axis=-1, keepdims=True) + NORM_EPS)
    return (rows_f * inv_rms * norm_gain.astype(F32)).astype(BF16)


def swiglu(rows_in, w_up, w_lin, w_down):
    gate_act = jnp.dot(rows_in, w_up, preferred_element_type=F32)
    lin_act = jnp.dot(rows_in, w_lin, preferred_element_type=F32)
    inner_act = (jax.nn.silu(gate_act) * lin_act).astype(BF16)
    return jnp.dot(inner_act, w_down, preferred_element_type=F32).astype(BF16)


def dense_path(n, hidden, norm_gain, w_gate, w1_shared, w3_shared, w2_shared, w1_experts, w3_experts, w2_experts, topk_ids):
    normed = rms_norm(hidden, norm_gain)
    probs = jax.nn.softmax(jnp.dot(normed, w_gate, preferred_element_type=F32), axis=-1)
    gate_wts = ROUTE_SCALE * jnp.take_along_axis(probs, topk_ids, axis=1)
    shared_out = swiglu(normed, w1_shared, w3_shared, w2_shared)
    pieces = 4
    width = normed.shape[1] // pieces
    gathered = [
        lax.all_gather(normed[:, i * width : (i + 1) * width], 'ep', axis=0, tiled=True) for i in range(pieces)
    ]
    all_rows = jnp.concatenate(gathered, axis=1)
    all_ids = lax.all_gather(topk_ids, 'ep', axis=0, tiled=True)
    all_wts = lax.all_gather(gate_wts, 'ep', axis=0, tiled=True)
    local_count = w1_experts.shape[0]
    first = lax.axis_index('ep') * local_count

    def one_expert(acc, xs):
        w_up, w_lin, w_down, expert = xs
        column = jnp.sum(jnp.where(all_ids == expert, all_wts, 0.0), axis=1)
        return acc + column[:, None] * swiglu(all_rows, w_up, w_lin, w_down).astype(F32), None

    part, _ = lax.scan(
        one_expert, jnp.zeros(all_rows.shape, F32), (w1_experts, w3_experts, w2_experts, first + jnp.arange(local_count))
    )
    back = lax.all_to_all(part.reshape(n, hidden.shape[0], -1), 'ep', split_axis=0, concat_axis=0)
    return (hidden.astype(F32) + shared_out.astype(F32) + jnp.sum(back, axis=0)).astype(BF16)


def moe_kernel(
    n, hid_hbm, gain_hbm, wg_hbm, w1s, w3s, w2s, w1e, w3e, w2e, ids_hbm,
    out_ref, most_ref,
    hid, gain, wg, ids, tile, info, wmap, rank, x_all, xg, gsel, ssel, wb, acc1, acc3, inner, ebuf,
    sacc1, sacc3, sinner, sh, part, from_sib, from_tr, from_fin, abuf, bbuf,
    in_sem, info_send, info_recv, ag_send, ag_recv, a_sem, b_sem,
    sib_send, sib_recv, tr_send, tr_recv, dir_send, com_send, fin_recv,
):
    rows, width = hid.shape
    experts, _, ff = w1e.shape
    total = n * rows
    chips = n // 2
    kd = width // K_CHUNKS
    jd = width // J_CHUNKS
    halves = w1s.shape[1] // ff
    n_shared = K_CHUNKS * halves
    n_up = K_CHUNKS * experts
    n_down = J_CHUNKS * experts
    n_down_all = n_down + J_CHUNKS * halves

    me = lax.axis_index('ep')
    chip, core = me // 2, lax.rem(me, 2)

    def dev(c, k):
        return lax.rem(c + chips, chips) * 2 + k

    right, left, sib = dev(chip + 1, core), dev(chip - 1, core), dev(chip, 1 - core)
    far = dev(chip + 2, core)

    def block(b):
        return pl.ds(pl.multiple_of(b * rows, 16), rows)

    small = [
        pltpu.make_async_copy(src, dst, in_sem.at[i])
        for i, (src, dst) in enumerate(((hid_hbm, hid), (gain_hbm, gain), (wg_hbm, wg), (ids_hbm, ids)))
    ]
    for copy in small:
        copy.start()

    def up_pair(pair, slot):
        return [pltpu.make_async_copy(src, abuf.at[slot, i], a_sem.at[slot, i]) for i, src in enumerate(pair)]

    def up_shared(s):
        k, h = s // halves, lax.rem(s, halves)
        at = (pl.ds(pl.multiple_of(k * kd, 128), kd), pl.ds(pl.multiple_of(h * ff, 128), ff))
        return up_pair((w1s.at[at], w3s.at[at]), lax.rem(s, UP_SLOTS))

    def up_routed(q):
        k, e = q // experts, lax.rem(q, experts)
        at = (e, pl.ds(pl.multiple_of(k * kd, 128), kd))
        return up_pair((w1e.at[at], w3e.at[at]), lax.rem(q + n_shared, UP_SLOTS))

    def down_routed(q):
        j, e = q // experts, lax.rem(q, experts)
        src = w2e.at[e, :, pl.ds(pl.multiple_of(j * jd, 128), jd)]
        slot = lax.rem(q, DOWN_SLOTS)
        return pltpu.make_async_copy(src, bbuf.at[slot], b_sem.at[slot])

    def down_shared(q):
        j, h = q // halves, lax.rem(q, halves)
        src = w2s.at[pl.ds(pl.multiple_of(h * ff, 128), ff), pl.ds(pl.multiple_of(j * jd, 128), jd)]
        slot = lax.rem(q + n_down, DOWN_SLOTS)
        return pltpu.make_async_copy(src, bbuf.at[slot], b_sem.at[slot])

    def start_up(s):
        if isinstance(s, int):
            if s < n_shared:
                for copy in up_shared(jnp.int32(s)):
                    copy.start()
            elif s < n_shared + n_up:
                for copy in up_routed(jnp.int32(s - n_shared)):
                    copy.start()
            return

        @pl.when(s < n_shared)
        def _():
            for copy in up_shared(s):
                copy.start()

        @pl.when((s >= n_shared) & (s < n_shared + n_up))
        def _():
            for copy in up_routed(s - n_shared):
                copy.start()

    def start_down(q):
        @pl.when(q < n_down)
        def _():
            down_routed(q).start()

        @pl.when((q >= n_down) & (q < n_down_all))
        def _():
            down_shared(q - n_down).start()

    for s in range(UP_SLOTS):
        start_up(s)
    for q in range(DOWN_SLOTS):
        down_routed(jnp.int32(q)).start()

    barrier = pltpu.get_barrier_semaphore()
    for i in range(1, n):
        pl.semaphore_signal(
            barrier, inc=1, device_id={'ep': lax.rem(me + i, n)}, device_id_type=pl.DeviceIdType.MESH
        )

    for copy in small:
        copy.wait()
    rows_f = hid[...].astype(F32)
    inv_rms = lax.rsqrt(jnp.mean(rows_f * rows_f, axis=-1, keepdims=True) + NORM_EPS)
    for k in range(K_CHUNKS):
        cols = slice(k * kd, (k + 1) * kd)
        x_all[k, block(me), :] = (rows_f[:, cols] * inv_rms * gain[:, cols].astype(F32)).astype(BF16)
    pl.semaphore_wait(barrier, n - 1)

    def remote(src, dst, send, recv, to):
        return pltpu.make_async_remote_copy(
            src_ref=src, dst_ref=dst, send_sem=send, recv_sem=recv, device_id={'ep': to}, device_id_type=pl.DeviceIdType.MESH
        )

    def rows_copy(k, b, lane, to):
        at = (k, block(b))
        return remote(x_all.at[at], x_all.at[at], ag_send.at[k, lane], ag_recv.at[k, b], to)

    def send_own(k):
        rows_copy(k, me, 0, right).start()
        rows_copy(k, me, 1, left).start()
        rows_copy(k, me, 2, sib).start()

    def forward_near(k):
        rows_copy(k, left, 3, sib).wait_recv()
        rows_copy(k, right, 4, sib).wait_recv()
        even = lax.rem(k, 2) == 0
        onward = jnp.where(even, left, right)
        to = jnp.where(even, right, left)
        rows_copy(k, onward, 5, to).start()
        rows_copy(k, left, 3, sib).start()
        rows_copy(k, right, 4, sib).start()

    def forward_far(k):
        rows_copy(k, far, 6, sib).wait_recv()
        rows_copy(k, far, 6, sib).start()

    def wait_sib_rows(k):
        for i in range(chips):
            rows_copy(k, dev(chip + i, 1 - core), 0, sib).wait_recv()

    send_own(0)
    send_own(1)

    logits = jnp.concatenate([x_all[k, block(me), :] for k in range(K_CHUNKS)], axis=1)
    logits = jnp.dot(logits, wg[...], preferred_element_type=F32)
    expd = jnp.exp(logits - jnp.max(logits, axis=-1, keepdims=True))
    probs = expd / jnp.sum(expd, axis=-1, keepdims=True)
    top_k = ids.shape[1]
    expert_lane = lax.broadcasted_iota(jnp.int32, probs.shape, 1)
    lane = lax.broadcasted_iota(jnp.int32, (rows, 128), 1)
    packed = jnp.zeros((rows, 128), F32)
    for i in range(top_k):
        col = ids[:, i : i + 1]
        wt = ROUTE_SCALE * jnp.sum(jnp.where(expert_lane == col, probs, 0.0), axis=-1, keepdims=True)
        packed = jnp.where(lane == i, wt, packed)
        packed = jnp.where(lane == 8 + i, col.astype(F32), packed)
    tile[...] = jnp.zeros_like(tile)
    tile[0:rows, :] = packed
    info[me] = tile[...].T[0:16, :]

    def info_copy(i, b, to):
        return remote(info.at[b], info.at[b], info_send.at[i], info_recv.at[b], to)

    def shared_step(s, _):
        k, h = s // halves, lax.rem(s, halves)
        for copy in up_shared(s):
            copy.wait()
        slot = lax.rem(s, UP_SLOTS)
        x = x_all[k, block(me), :]
        for i, acc in enumerate((sacc1, sacc3)):
            d = jnp.dot(x, abuf[slot, i], preferred_element_type=F32)

            @pl.when(k == 0)
            def _():
                acc[h] = d

            @pl.when(k > 0)
            def _():
                acc[h] = acc[h] + d

        start_up(s + UP_SLOTS)

        @pl.when(s == 0)
        def _():
            for i in range(1, n):
                info_copy(i, me, lax.rem(me + i, n)).start()

        @pl.when(s == 3)
        def _():
            forward_near(jnp.int32(0))
            send_own(jnp.int32(2))

        @pl.when(s == 6)
        def _():
            forward_near(jnp.int32(1))
            send_own(jnp.int32(3))

        return 0

    lax.fori_loop(0, n_shared, shared_step, 0)

    for i in range(1, n):
        b = lax.rem(me + i, n)
        info_copy(i, b, b).wait_recv()
    info_cols = info[...].reshape(n * 16, 128).T
    first = (me * experts).astype(F32)
    all_experts = float(n * experts)
    lane_f = lax.broadcasted_iota(jnp.int32, (rows, 128), 1).astype(F32)
    lower = lax.broadcasted_iota(jnp.int32, (rows, rows), 0) > lax.broadcasted_iota(jnp.int32, (rows, rows), 1)
    lower = jnp.where(lower, 1.0, 0.0).astype(BF16)
    seen = jnp.zeros((1, 128), F32)
    for b in range(n):
        wm = jnp.zeros((rows, 128), F32)
        hit_any = jnp.zeros((rows, 128), F32)
        for i in range(top_k):
            wt = info_cols[0:rows, 16 * b + i : 16 * b + i + 1]
            at = info_cols[0:rows, 16 * b + 8 + i : 16 * b + 9 + i] - first
            at = jnp.where(at < 0, at + all_experts, at)
            hit = lane_f == at
            wm = jnp.where(hit, wt, wm)
            hit_any = jnp.where(hit, 1.0, hit_any)
        before = jnp.dot(lower, hit_any.astype(BF16), preferred_element_type=F32) + seen
        wmap[b * rows : (b + 1) * rows, :] = wm
        rank[b * rows : (b + 1) * rows, :] = jnp.where(hit_any > 0, before, -1.0)
        seen = seen + jnp.sum(hit_any, axis=0, keepdims=True)
    most_ref[...] = jnp.broadcast_to(jnp.max(seen, axis=1, keepdims=True), most_ref.shape)
    rank_rows = rank[...].T
    place = lax.broadcasted_iota(jnp.int32, (CAP, total), 0).astype(F32)
    for e in range(experts):
        hit = place == jnp.broadcast_to(rank_rows[e : e + 1, :], (CAP, total))
        gsel[e * CAP : (e + 1) * CAP, :] = jnp.where(hit, 1.0, 0.0).astype(BF16)

    forward_far(jnp.int32(0))

    def up_chunk(k, _):
        wait_sib_rows(k)
        for half in range(2):
            span = slice(half * experts * CAP // 2, (half + 1) * experts * CAP // 2)
            xg[span, :] = jnp.dot(gsel[span, :], x_all[k], preferred_element_type=F32).astype(BF16)

        def up_step(e, _):
            q = k * experts + e
            for copy in up_routed(q):
                copy.wait()
            slot = lax.rem(q + n_shared, UP_SLOTS)
            x = xg[pl.ds(pl.multiple_of(e * CAP, CAP), CAP), :]
            for i, acc in enumerate((acc1, acc3)):
                d = jnp.dot(x, abuf[slot, i], preferred_element_type=F32)

                @pl.when(k == 0)
                def _():
                    acc[e] = d

                @pl.when(k > 0)
                def _():
                    acc[e] = acc[e] + d

            start_up(q + n_shared + UP_SLOTS)

            @pl.when((e == 3) & (k + 1 < K_CHUNKS))
            def _():
                forward_far(k + 1)

            @pl.when((e == 3) & (k + 2 < K_CHUNKS))
            def _():
                forward_near(k + 2)

            return 0

        lax.fori_loop(0, experts, up_step, 0)

        @pl.when(k == 1)
        def _():
            slots = lax.broadcasted_iota(jnp.int32, (total, CAP), 1).astype(F32)
            ranks = rank[...]
            wts = wmap[...]
            for e in range(experts):
                hit = slots == jnp.broadcast_to(ranks[:, e : e + 1], (total, CAP))
                ssel[e] = jnp.where(hit, 1.0, 0.0).astype(BF16)
                wb[e] = jnp.broadcast_to(wts[:, e : e + 1], (total, 128))

        return 0

    lax.fori_loop(0, K_CHUNKS, up_chunk, 0)

    def activate(e, _):
        inner[e] = (jax.nn.silu(acc1[e]) * acc3[e]).astype(BF16)
        return 0

    lax.fori_loop(0, experts, activate, 0)
    for h in range(halves):
        sinner[h] = (jax.nn.silu(sacc1[h]) * sacc3[h]).astype(BF16)

    def sib_copy(j, c):
        return remote(
            part.at[j, block(c * 2 + (1 - core))], from_sib.at[j, c], sib_send.at[j, c], sib_recv.at[j, c], sib
        )

    def step_of(j):
        return 1 - 2 * lax.rem(j, 2)

    def tr_copy(j):
        d = step_of(j)
        return remote(part.at[j, block(far)], from_tr.at[j], tr_send.at[j], tr_recv.at[j], dev(chip + d, core))

    def dir_copy(j):
        to = dev(chip - step_of(j), core)
        return remote(part.at[j, block(to)], from_fin.at[1, j], dir_send.at[j], fin_recv.at[1, j], to)

    def com_copy(j):
        to = dev(chip + step_of(j), core)
        return remote(part.at[j, block(to)], from_fin.at[0, j], com_send.at[j], fin_recv.at[0, j], to)

    def down_range(j, _):
        @pl.when(j < J_CHUNKS)
        def _():
            def down_step(g, _):
                for u in range(4):
                    e = g * 4 + u
                    q = j * experts + e
                    down_routed(q).wait()
                    d = jnp.dot(inner[e], bbuf[lax.rem(q, DOWN_SLOTS)], preferred_element_type=F32)
                    ebuf[e] = d.astype(BF16)
                for u in range(4):
                    start_down(j * experts + g * 4 + u + DOWN_SLOTS)
                return 0

            lax.fori_loop(0, experts // 4, down_step, 0)

            def spread(m, _):
                span = pl.ds(pl.multiple_of(m * 128, 128), 128)
                acc = jnp.zeros((128, jd), F32)
                for e in range(experts):
                    d = jnp.dot(ssel[e, span, :], ebuf[e], preferred_element_type=F32)
                    wt = wb[e, span, :]
                    if jd > 128:
                        wt = jnp.concatenate([wt] * (jd // 128), axis=1)
                    elif jd < 128:
                        wt = wt[:, :jd]
                    acc = acc + d * wt
                part[j, span, :] = acc
                return 0

            lax.fori_loop(0, total // 128, spread, 0)

        @pl.when((j >= 1) & (j <= J_CHUNKS))
        def _():
            for c in range(chips):
                sib_copy(j - 1, c).wait_recv()
                at = (j - 1, block(c * 2 + core))
                part[at] = part[at] + from_sib[j - 1, c]

        @pl.when(j >= LAG)
        def _():
            i = j - LAG
            tr_copy(i).wait_recv()
            at = (i, block(dev(chip + step_of(i), core)))
            part[at] = part[at] + from_tr[i]

        @pl.when((j >= 1) & (j <= J_CHUNKS))
        def _():
            dir_copy(j - 1).start()
            tr_copy(j - 1).start()

        @pl.when(j >= LAG)
        def _():
            com_copy(j - LAG).start()

        @pl.when(j < J_CHUNKS)
        def _():
            for c in range(chips):
                sib_copy(j, c).start()

        return 0

    lax.fori_loop(0, J_CHUNKS + LAG, down_range, 0)

    def shared_down(j, _):
        acc = jnp.zeros((rows, jd), F32)
        for h in range(halves):
            q = j * halves + h
            down_shared(q).wait()
            acc = acc + jnp.dot(sinner[h], bbuf[lax.rem(q + n_down, DOWN_SLOTS)], preferred_element_type=F32)
        sh[j] = acc
        for h in range(halves):
            start_down(n_down + j * halves + h + DOWN_SLOTS)
        return 0

    lax.fori_loop(0, J_CHUNKS, shared_down, 0)

    for j in range(J_CHUNKS):
        cols = slice(j * jd, (j + 1) * jd)
        com_copy(jnp.int32(j)).wait_recv()
        dir_copy(jnp.int32(j)).wait_recv()
        routed = part[j, block(me), :] + (from_fin[0, j] + from_fin[1, j])
        shared_out = sh[j].astype(BF16).astype(F32)
        out_ref[:, cols] = (hid[:, cols].astype(F32) + shared_out + routed).astype(BF16)

    for i in range(1, n):
        info_copy(i, me, lax.rem(me + i, n)).wait_send()
    for k in range(K_CHUNKS):
        for lane_i in range(7):
            rows_copy(jnp.int32(k), me, lane_i, sib).wait_send()
    for j in range(J_CHUNKS):
        ji = jnp.int32(j)
        for c in range(chips):
            sib_copy(ji, c).wait_send()
        tr_copy(ji).wait_send()
        dir_copy(ji).wait_send()
        com_copy(ji).wait_send()


def routed_layer(n, *args):
    hidden, norm_gain, w_gate, w1_shared, w3_shared, w2_shared, w1_experts, w3_experts, w2_experts, topk_ids = args
    rows, width = hidden.shape
    experts, _, ff = w1_experts.shape
    total = n * rows
    chips = n // 2
    kd = width // K_CHUNKS
    jd = width // J_CHUNKS
    halves = w1_shared.shape[1] // ff
    dma = pltpu.SemaphoreType.DMA
    vmem = pltpu.VMEM
    scratch = [
        vmem((rows, width), BF16),
        vmem((1, width), BF16),
        vmem(w_gate.shape, BF16),
        vmem(topk_ids.shape, jnp.int32),
        vmem((128, 128), F32),
        vmem((n, 16, 128), F32),
        vmem((total, 128), F32),
        vmem((total, 128), F32),
        vmem((K_CHUNKS, total, kd), BF16),
        vmem((experts * CAP, kd), BF16),
        vmem((experts * CAP, total), BF16),
        vmem((experts, total, CAP), BF16),
        vmem((experts, total, 128), F32),
        vmem((experts, CAP, ff), F32),
        vmem((experts, CAP, ff), F32),
        vmem((experts, CAP, ff), BF16),
        vmem((experts, CAP, jd), BF16),
        vmem((halves, rows, ff), F32),
        vmem((halves, rows, ff), F32),
        vmem((halves, rows, ff), BF16),
        vmem((J_CHUNKS, rows, jd), F32),
        vmem((J_CHUNKS, total, jd), F32),
        vmem((J_CHUNKS, chips, rows, jd), F32),
        vmem((J_CHUNKS, rows, jd), F32),
        vmem((2, J_CHUNKS, rows, jd), F32),
        vmem((UP_SLOTS, 2, kd, ff), BF16),
        vmem((DOWN_SLOTS, ff, jd), BF16),
        dma((4,)),
        dma((n,)),
        dma((n,)),
        dma((K_CHUNKS, 7)),
        dma((K_CHUNKS, n)),
        dma((UP_SLOTS, 2)),
        dma((DOWN_SLOTS,)),
        dma((J_CHUNKS, chips)),
        dma((J_CHUNKS, chips)),
        dma((J_CHUNKS,)),
        dma((J_CHUNKS,)),
        dma((J_CHUNKS,)),
        dma((J_CHUNKS,)),
        dma((2, J_CHUNKS)),
    ]
    return pl.pallas_call(
        functools.partial(moe_kernel, n),
        out_shape=[jax.ShapeDtypeStruct((rows, width), BF16), jax.ShapeDtypeStruct((8, 128), F32)],
        in_specs=[pl.BlockSpec(memory_space=pl.ANY)] * 10,
        out_specs=[pl.BlockSpec(memory_space=pltpu.VMEM)] * 2,
        scratch_shapes=scratch,
        compiler_params=pltpu.CompilerParams(collective_id=0, has_side_effects=True, vmem_limit_bytes=67043328),
        name='moe_layer',
    )(hidden, norm_gain.reshape(1, width), *args[2:])


def solution(mesh):
    n = mesh.shape['ep']
    tok_spec = P(('dp', 'ep'), None)
    expert_spec = P('ep', None, None)

    def local_fn(*args):
        out, most = routed_layer(n, *args)
        return lax.cond(most[0, 0] > CAP, lambda: dense_path(n, *args), lambda: out)

    return jax.shard_map(local_fn, mesh=mesh, in_specs=(tok_spec, P(), P(), P(), P(), P(), expert_spec, expert_spec, expert_spec, tok_spec), out_specs=tok_spec, check_vma=False)
```

time: 257 us -> 120 us (0.47)
  matrix products: 170 us -> 0 us
  Pallas kernels: 0 us -> 111 us
  waiting for transfers between devices: 34.9 us -> 0 us
  blocking collectives: 28 us -> 0 us
  between operations: 13.6 us -> 0.67 us
  other arithmetic: 5.27 us -> 0 us
  local copies, waits for them, and re-layouts: 4.69 us -> 7.59 us
    dot_general x6 -> x0, matrix products: 170 us -> none  [the longest x1 52.7 us: routed_experts(): jnp.einsum('nd,edf->enf', rows_in, w1_experts, preferred_element_type=jnp...]
    pallas_call x0 -> x1, Pallas kernels: none -> 111 us  [routed_layer(): pl.pallas_call(functools.partial(moe_kernel, n), out_shape=[jax.ShapeDtyp...]
    reduce_scatter x1 -> x0, waiting for transfers between devices: 34.8 us -> none  [local_fn(): routed = lax.psum_scatter(part_sum, 'ep', scatter_dimension=0, tiled=True)]
    all_gather x2 -> x0, blocking collectives: 28 us -> none  [the longest x1 14.9 us: local_fn(): all_wts = lax.all_gather(gate_wts, 'ep', axis=0, tiled=True)]
    unnamed x22 -> x3, local copies, waits for them, and re-layouts: 0.2 us -> 5.11 us
    gather x5 -> x0, local copies, waits for them, and re-layouts: 4.47 us -> none  [router_weights(): return ROUTE_SCALE * jnp.take_along_axis(gate_probs, topk_ids, axis=1)]
    convert_element_type x2 -> x0, other arithmetic: 2.64 us -> none  [the longest x1 1.9 us: rms_norm(): (rows_f * inv_rms * norm_gain.astype(jnp.float32)).astype(jnp.bfloat16)]
  transfers between devices with their start and end apart: 2 -> 0, of which waited for: 1 -> 0; matrix products, arithmetic and copies ran while one was open for 5% -> 0% of each run, Pallas kernels for 0% -> 0%
where the time goes in v1:
time: 120 us
  Pallas kernels  111 us (92%)
  local copies, waits for them, and re-layouts  7.59 us (6%)
    pallas_call x1, Pallas kernels, routed_layer(): pl.pallas_call(functools.partial(moe_kernel, n), out_shape=[jax.ShapeDtyp...  111 us
    unnamed x3, local copies, waits for them, and re-layouts  5.11 us

profile of v1, /device:TPU:81, one launch (start us, length us, event | category | flops | bytes accessed | tf_op | source)
XLA Modules:
  0.0 119.8 jit_solution(13634336249257434920)
XLA Ops:
  0.0 1.9 %copy.34.wg_hbm = bf16[2048,64]{1,0:T(8,128)(2,1)} copy(bf16[2048,64]{0,1:T(8,128)(2,1)} %param.16) | data formatting | bytes 524288 | tf_op args[2]
  1.9 1.4 %copy.35.ids_hbm = s32[96,6]{1,0:T(8,128)} copy(s32[96,6]{0,1:T(8,128)} %param.23) | data formatting | bytes 4608 | tf_op args[9]
  3.3 1.3 %reshape.31.gain_hbm = bf16[1,2048]{1,0:T(2,128)(2,1)} reshape(bf16[2048]{0:T(1024)(128)(2,1)} %param.15) | data formatting | bytes 8192 | tf_op jit(solution)/shard_map/reshape | solution.py:543
  4.6 111.3 %moe_layer.1 = (bf16[96,2048]{1,0:T(8,128)(2,1)}, f32[8,128]{1,0:T(8,128)}) custom-call(bf16[96,2048]{1,0:T(8,128)(2,1)} %hid_hbm.1, bf16[1,2048]{1,0:T(2,128)(2,1)} %reshape.31.gain_hbm, bf16[2048,64]{1,0:T(8,128)(2,1)} %copy.34.wg_hbm, bf16[2048,2816]{1,0:T(8,128)(2,1)} %w1s.1, bf16[2048,2816]{1,0:T(8,128)(2,1)} %w3s.1, bf16[2816,2048]{1,0:T(8,128)(2,1)} %w2s.1, ...), custom_call_target="tpu_custom_call" | custom-call | tf_op jit(solution)/shard_map/moe_layer/pallas_call | solution.py:535
  115.9 1.2 slice.15
  117.8 0.2 conditional.1
  118.0 1.8 %copy.48 = bf16[96,2048]{1,0:T(8,128)(2,1)} copy(bf16[96,2048]{1,0:T(8,128)(2,1)} %get-tuple-element.90) | data formatting | bytes 786432

commit v2 on v0

v2 whole, which is shorter than its diff:
```python
import functools

import jax
import jax.numpy as jnp
from jax import lax
from jax.experimental import pallas as pl
from jax.experimental.pallas import tpu as pltpu
from jax.sharding import PartitionSpec as P

ROUTE_SCALE = 16
NORM_EPS = 1e-6
CAP = 128
K_CHUNKS = 4
J_CHUNKS = 8
N_CHUNKS = 4
UP_SLOTS = 7

F32 = jnp.float32
BF16 = jnp.bfloat16


def rms_norm(hidden, norm_gain):
    rows_f = hidden.astype(F32)
    inv_rms = lax.rsqrt(jnp.mean(rows_f * rows_f, axis=-1, keepdims=True) + NORM_EPS)
    return (rows_f * inv_rms * norm_gain.astype(F32)).astype(BF16)


def swiglu(rows_in, w_up, w_lin, w_down):
    gate_act = jnp.dot(rows_in, w_up, preferred_element_type=F32)
    lin_act = jnp.dot(rows_in, w_lin, preferred_element_type=F32)
    inner_act = (jax.nn.silu(gate_act) * lin_act).astype(BF16)
    return jnp.dot(inner_act, w_down, preferred_element_type=F32).astype(BF16)


def dense_path(n, hidden, norm_gain, w_gate, w1_shared, w3_shared, w2_shared, w1_experts, w3_experts, w2_experts, topk_ids):
    normed = rms_norm(hidden, norm_gain)
    probs = jax.nn.softmax(jnp.dot(normed, w_gate, preferred_element_type=F32), axis=-1)
    gate_wts = ROUTE_SCALE * jnp.take_along_axis(probs, topk_ids, axis=1)
    shared_out = swiglu(normed, w1_shared, w3_shared, w2_shared)
    pieces = 4
    width = normed.shape[1] // pieces
    gathered = [
        lax.all_gather(normed[:, i * width : (i + 1) * width], 'ep', axis=0, tiled=True) for i in range(pieces)
    ]
    all_rows = jnp.concatenate(gathered, axis=1)
    all_ids = lax.all_gather(topk_ids, 'ep', axis=0, tiled=True)
    all_wts = lax.all_gather(gate_wts, 'ep', axis=0, tiled=True)
    local_count = w1_experts.shape[0]
    first = lax.axis_index('ep') * local_count

    def one_expert(acc, xs):
        w_up, w_lin, w_down, expert = xs
        column = jnp.sum(jnp.where(all_ids == expert, all_wts, 0.0), axis=1)
        return acc + column[:, None] * swiglu(all_rows, w_up, w_lin, w_down).astype(F32), None

    part, _ = lax.scan(
        one_expert, jnp.zeros(all_rows.shape, F32), (w1_experts, w3_experts, w2_experts, first + jnp.arange(local_count))
    )
    back = lax.all_to_all(part.reshape(n, hidden.shape[0], -1), 'ep', split_axis=0, concat_axis=0)
    return (hidden.astype(F32) + shared_out.astype(F32) + jnp.sum(back, axis=0)).astype(BF16)


def moe_kernel(
    n, hid_hbm, gain_hbm, wg_hbm, w1s, w3s, w2s, w1e, w3e, w2e, ids_hbm,
    out_ref, over_ref,
    hid, gain, wg, ids, tile, info, wmap, rank, x_all, ssel, wb, inner, sinner, sh,
    from_sib, from_tr, from_fin, bbuf,
    in_sem, info_send, info_recv, ag_send, ag_recv, a_sem, b_sem,
    sib_send, sib_recv, tr_send, tr_recv, dir_send, com_send, fin_recv,
):
    rows, width = hid.shape
    experts, _, ff = w1e.shape
    total = n * rows
    chips = n // 2
    kd = width // K_CHUNKS
    jd = width // J_CHUNKS
    nd = width // N_CHUNKS
    per = nd // jd
    halves = w1s.shape[1] // ff
    n_shared = K_CHUNKS * halves
    n_up = K_CHUNKS * experts
    slots = experts // 2

    me = lax.axis_index('ep')
    chip, core = me // 2, lax.rem(me, 2)

    def dev(c, k):
        return lax.rem(c + chips, chips) * 2 + k

    right, left, sib = dev(chip + 1, core), dev(chip - 1, core), dev(chip, 1 - core)
    far = dev(chip + 2, core)

    def block(b):
        return pl.ds(pl.multiple_of(b * rows, 16), rows)

    small = [
        pltpu.make_async_copy(src, dst, in_sem.at[i])
        for i, (src, dst) in enumerate(((hid_hbm, hid), (gain_hbm, gain), (wg_hbm, wg), (ids_hbm, ids)))
    ]
    for copy in small:
        copy.start()

    def down_routed(t, e, buf, slot, sem):
        src = w2e.at[e, :, pl.ds(pl.multiple_of(t * nd, 128), nd)]
        return pltpu.make_async_copy(src, buf.at[slot], b_sem.at[sem])

    def down_shared(q, buf, slot, sem):
        t, h = q // halves, lax.rem(q, halves)
        src = w2s.at[pl.ds(pl.multiple_of(h * ff, 128), ff), pl.ds(pl.multiple_of(t * nd, 128), nd)]
        return pltpu.make_async_copy(src, buf.at[slot], b_sem.at[sem])

    barrier = pltpu.get_barrier_semaphore()
    for i in range(1, n):
        pl.semaphore_signal(
            barrier, inc=1, device_id={'ep': lax.rem(me + i, n)}, device_id_type=pl.DeviceIdType.MESH
        )

    def remote(src, dst, send, recv, to):
        return pltpu.make_async_remote_copy(
            src_ref=src, dst_ref=dst, send_sem=send, recv_sem=recv, device_id={'ep': to}, device_id_type=pl.DeviceIdType.MESH
        )

    def phase_one(xg, gsel, acc1, acc3, sacc1, sacc3, abuf):
        def up_pair(pair, slot):
            return [pltpu.make_async_copy(src, abuf.at[slot, i], a_sem.at[slot, i]) for i, src in enumerate(pair)]

        def up_shared(s):
            k, h = s // halves, lax.rem(s, halves)
            at = (pl.ds(pl.multiple_of(k * kd, 128), kd), pl.ds(pl.multiple_of(h * ff, 128), ff))
            return up_pair((w1s.at[at], w3s.at[at]), lax.rem(s, UP_SLOTS))

        def up_routed(q):
            k, e = q // experts, lax.rem(q, experts)
            at = (e, pl.ds(pl.multiple_of(k * kd, 128), kd))
            return up_pair((w1e.at[at], w3e.at[at]), lax.rem(q + n_shared, UP_SLOTS))

        def start_up(s):
            if isinstance(s, int):
                if s < n_shared:
                    for copy in up_shared(jnp.int32(s)):
                        copy.start()
                elif s < n_shared + n_up:
                    for copy in up_routed(jnp.int32(s - n_shared)):
                        copy.start()
                return

            @pl.when(s < n_shared)
            def _():
                for copy in up_shared(s):
                    copy.start()

            @pl.when((s >= n_shared) & (s < n_shared + n_up))
            def _():
                for copy in up_routed(s - n_shared):
                    copy.start()

        with jax.named_scope('small_in'):
            for copy in small:
                copy.wait()
        for s in range(UP_SLOTS):
            start_up(s)
        for e in range(experts // 2):
            down_routed(0, e, bbuf, e, e).start()
        with jax.named_scope('norm'):
            rows_f = hid[...].astype(F32)
            inv_rms = lax.rsqrt(jnp.mean(rows_f * rows_f, axis=-1, keepdims=True) + NORM_EPS)
            for k in range(K_CHUNKS):
                cols = slice(k * kd, (k + 1) * kd)
                x_all[k, block(me), :] = (rows_f[:, cols] * inv_rms * gain[:, cols].astype(F32)).astype(BF16)
        with jax.named_scope('barrier'):
            pl.semaphore_wait(barrier, n - 1)

        def rows_copy(k, b, lane, to):
            at = (k, block(b))
            return remote(x_all.at[at], x_all.at[at], ag_send.at[k, lane], ag_recv.at[k, b], to)

        def send_own(k):
            rows_copy(k, me, 0, right).start()
            rows_copy(k, me, 1, left).start()
            rows_copy(k, me, 2, sib).start()

        def forward_near(k):
            rows_copy(k, left, 3, sib).wait_recv()
            rows_copy(k, right, 4, sib).wait_recv()
            even = lax.rem(k, 2) == 0
            onward = jnp.where(even, left, right)
            to = jnp.where(even, right, left)
            rows_copy(k, onward, 5, to).start()
            rows_copy(k, left, 3, sib).start()
            rows_copy(k, right, 4, sib).start()

        def forward_far(k):
            rows_copy(k, far, 6, sib).wait_recv()
            rows_copy(k, far, 6, sib).start()

        def wait_sib_rows(k):
            for i in range(chips):
                rows_copy(k, dev(chip + i, 1 - core), 0, sib).wait_recv()

        send_own(0)
        send_own(1)

        logits = jnp.concatenate([x_all[k, block(me), :] for k in range(K_CHUNKS)], axis=1)
        logits = lax.dot_general(logits, wg[...], (((1,), (1,)), ((), ())), preferred_element_type=F32)
        expd = jnp.exp(logits - jnp.max(logits, axis=-1, keepdims=True))
        probs = expd / jnp.sum(expd, axis=-1, keepdims=True)
        top_k = ids.shape[0]
        tile[...] = jnp.zeros_like(tile)
        tile[0:top_k, 0:rows] = ids[...].astype(F32)
        id_cols = tile[...].T[0:rows, :]
        expert_lane = lax.broadcasted_iota(jnp.int32, probs.shape, 1).astype(F32)
        lane = lax.broadcasted_iota(jnp.int32, (rows, 128), 1)
        packed = jnp.zeros((rows, 128), F32)
        for i in range(top_k):
            col = id_cols[:, i : i + 1]
            wt = ROUTE_SCALE * jnp.sum(jnp.where(expert_lane == col, probs, 0.0), axis=-1, keepdims=True)
            packed = jnp.where(lane == i, wt, packed)
            packed = jnp.where(lane == 8 + i, col, packed)
        tile[...] = jnp.zeros_like(tile)
        tile[0:rows, :] = packed
        info[me] = tile[...].T[0:16, :]

        def info_copy(i, b, to):
            return remote(info.at[b], info.at[b], info_send.at[i], info_recv.at[b], to)

        def shared_step(s, _):
            k, h = s // halves, lax.rem(s, halves)
            for copy in up_shared(s):
                copy.wait()
            slot = lax.rem(s, UP_SLOTS)
            x = x_all[k, block(me), :]
            for i, acc in enumerate((sacc1, sacc3)):
                d = jnp.dot(x, abuf[slot, i], preferred_element_type=F32)
                acc[h] = d + jnp.where(k == 0, 0.0, acc[h])

            start_up(s + UP_SLOTS)

            @pl.when(s == 0)
            def _():
                for i in range(1, n):
                    info_copy(i, me, lax.rem(me + i, n)).start()

            @pl.when(s == 3)
            def _():
                forward_near(jnp.int32(0))
                send_own(jnp.int32(2))

            @pl.when(s == 6)
            def _():
                forward_near(jnp.int32(1))
                send_own(jnp.int32(3))

            return 0

        with jax.named_scope('shared_up'):
            lax.fori_loop(0, n_shared, shared_step, 0)

        for i in range(1, n):
            b = lax.rem(me + i, n)
            info_copy(i, b, b).wait_recv()
        info_cols = info[...].reshape(n * 16, 128).T
        first = (me * experts).astype(F32)
        all_experts = float(n * experts)
        lane_f = lax.broadcasted_iota(jnp.int32, (rows, 128), 1).astype(F32)
        lower = lax.broadcasted_iota(jnp.int32, (rows, rows), 0) > lax.broadcasted_iota(jnp.int32, (rows, rows), 1)
        lower = jnp.where(lower, 1.0, 0.0).astype(BF16)
        seen = jnp.zeros((1, 128), F32)
        for b in range(n):
            wm = jnp.zeros((rows, 128), F32)
            hit_any = jnp.zeros((rows, 128), F32)
            for i in range(top_k):
                wt = info_cols[0:rows, 16 * b + i : 16 * b + i + 1]
                at = info_cols[0:rows, 16 * b + 8 + i : 16 * b + 9 + i] - first
                at = jnp.where(at < 0, at + all_experts, at)
                hit = lane_f == at
                wm = jnp.where(hit, wt, wm)
                hit_any = jnp.where(hit, 1.0, hit_any)
            before = jnp.dot(lower, hit_any.astype(BF16), preferred_element_type=F32) + seen
            wmap[b * rows : (b + 1) * rows, :] = wm
            rank[b * rows : (b + 1) * rows, :] = jnp.where(hit_any > 0, before, -1.0)
            seen = seen + jnp.sum(hit_any, axis=0, keepdims=True)
        over_ref[0, 0] = (jnp.max(seen) > CAP).astype(jnp.int32)
        rank_rows = rank[...].T
        place = lax.broadcasted_iota(jnp.int32, (CAP, total), 0).astype(F32)
        for e in range(experts):
            hit = place == jnp.broadcast_to(rank_rows[e : e + 1, :], (CAP, total))
            gsel[e * CAP : (e + 1) * CAP, :] = jnp.where(hit, 1.0, 0.0).astype(BF16)

        forward_far(jnp.int32(0))

        def up_chunk(k, _):
            with jax.named_scope('wait_rows'):
                wait_sib_rows(k)
            for half in range(2):
                span = slice(half * experts * CAP // 2, (half + 1) * experts * CAP // 2)
                xg[span, :] = jnp.dot(gsel[span, :], x_all[k], preferred_element_type=F32).astype(BF16)

            def up_step(e, _):
                q = k * experts + e
                for copy in up_routed(q):
                    copy.wait()
                slot = lax.rem(q + n_shared, UP_SLOTS)
                x = xg[pl.ds(pl.multiple_of(e * CAP, CAP), CAP), :]
                for i, acc in enumerate((acc1, acc3)):
                    d = jnp.dot(x, abuf[slot, i], preferred_element_type=F32)
                    acc[e] = d + jnp.where(k == 0, 0.0, acc[e])

                start_up(q + n_shared + UP_SLOTS)

                for i in range(experts):

                    @pl.when((k == 1) & (e == i))
                    def _():
                        slots = lax.broadcasted_iota(jnp.int32, (total, CAP), 1).astype(F32)
                        hit = slots == jnp.broadcast_to(rank[:, i : i + 1], (total, CAP))
                        ssel[i] = jnp.where(hit, 1.0, 0.0).astype(BF16)
                        wb[i] = jnp.broadcast_to(wmap[:, i : i + 1], (total, 128))

                @pl.when((e == 3) & (k + 1 < K_CHUNKS))
                def _():
                    forward_far(k + 1)

                @pl.when((e == 3) & (k + 2 < K_CHUNKS))
                def _():
                    forward_near(k + 2)

                return 0

            with jax.named_scope('up_steps'):
                lax.fori_loop(0, experts, up_step, 0)

            return 0

        lax.fori_loop(0, K_CHUNKS, up_chunk, 0)

        def activate(e, _):
            inner[e] = (jax.nn.silu(acc1[e]) * acc3[e]).astype(BF16)
            return 0

        with jax.named_scope('act'):
            lax.fori_loop(0, experts, activate, 0)
        for h in range(halves):
            sinner[h] = (jax.nn.silu(sacc1[h]) * sacc3[h]).astype(BF16)
        for i in range(1, n):
            info_copy(i, me, lax.rem(me + i, n)).wait_send()
        for k in range(K_CHUNKS):
            for lane_i in range(7):
                rows_copy(jnp.int32(k), me, lane_i, sib).wait_send()

    def phase_two(ebuf, part, bbuf_hi):
        for e in range(slots):
            down_routed(0, slots + e, bbuf_hi, e, slots + e).start()
        def sib_copy(j, c):
            return remote(
                part.at[j, block(c * 2 + (1 - core))], from_sib.at[j, c], sib_send.at[j, c], sib_recv.at[j, c], sib
            )

        def step_of(j):
            return 1 - 2 * lax.rem(j, 2)

        def tr_copy(j):
            d = step_of(j)
            return remote(part.at[j, block(far)], from_tr.at[j], tr_send.at[j], tr_recv.at[j], dev(chip + d, core))

        def dir_copy(j):
            to = dev(chip - step_of(j), core)
            return remote(part.at[j, block(to)], from_fin.at[1, j], dir_send.at[j], fin_recv.at[1, j], to)

        def com_copy(j):
            to = dev(chip + step_of(j), core)
            return remote(part.at[j, block(to)], from_fin.at[0, j], com_send.at[j], fin_recv.at[0, j], to)

        def products(t, half):
            buf = (bbuf, bbuf_hi)[half]

            def down_step(g, _):
                for u in range(2):
                    slot = g * 2 + u
                    e = half * slots + slot
                    down_routed(t, e, buf, slot, e).wait()
                    d = jnp.dot(inner[e], buf[slot], preferred_element_type=F32)
                    ebuf[t, e] = d.astype(BF16)
                for u in range(2):
                    slot = g * 2 + u
                    e = half * slots + slot

                    @pl.when(t + 1 < N_CHUNKS)
                    def _():
                        down_routed(t + 1, e, buf, slot, e).start()

                    @pl.when(t + 1 == N_CHUNKS)
                    def _():
                        down_shared(e, buf, slot, e).start()

                return 0

            with jax.named_scope('products'):
                lax.fori_loop(0, slots // 2, down_step, 0)

        def spread(t, c):
            span = pl.ds(pl.multiple_of(c * 2 * rows, 32), 2 * rows)
            with jax.named_scope('spread'):
                acc = jnp.zeros((2 * rows, nd), F32)
                for e in range(experts):
                    d = jnp.dot(ssel[e, span, :], ebuf[t, e], preferred_element_type=F32)
                    wt = wb[e, span, :]
                    if nd > 128:
                        wt = jnp.concatenate([wt] * (nd // 128), axis=1)
                    acc = acc + d * wt
                for i in range(per):
                    part[t * per + i, span, :] = acc[:, i * jd : (i + 1) * jd]
            for i in range(per):
                sib_copy(t * per + i, c).start()

        def shared_down(i, half):
            buf = (bbuf, bbuf_hi)[half]
            t = half * (N_CHUNKS // 2) + i
            with jax.named_scope('shared_down'):
                acc = jnp.zeros((rows, nd), F32)
                for h in range(halves):
                    slot = i * halves + h
                    q = half * slots + slot
                    down_shared(q, buf, slot, q).wait()
                    acc = acc + jnp.dot(sinner[h], buf[slot], preferred_element_type=F32)
                for k in range(per):
                    sh[t * per + k] = acc[:, k * jd : (k + 1) * jd]

        def add_sib(t, c):
            with jax.named_scope('add_sib'):
                for i in range(per):
                    j = t * per + i
                    sib_copy(j, c).wait_recv()
                    at = (j, block(c * 2 + core))
                    part[at] = part[at] + from_sib[j, c]

        def near_home(t):
            add_sib(t, chip_right)
            add_sib(t, chip_left)
            for i in range(per):
                dir_copy(t * per + i).start()

        def far_onward(t):
            add_sib(t, chip_far)
            for i in range(per):
                tr_copy(t * per + i).start()

        def far_home(t):
            for i in range(per):
                j = t * per + i
                with jax.named_scope('add_tr'):
                    tr_copy(j).wait_recv()
                    at = (j, block(dev(chip + step_of(j), core)))
                    part[at] = part[at] + from_tr[j]
                com_copy(j).start()

        chip_right, chip_left, chip_far = (lax.rem(chip + i, chips) for i in (1, chips - 1, 2))

        def down_range(t, _):
            products(t, 0)

            @pl.when(t >= 1)
            def _():
                near_home(t - 1)

            products(t, 1)

            def three(i, _):
                spread(t, lax.rem(chip + 2 - i + 3 * (i // 2), chips))
                return 0

            lax.fori_loop(0, 3, three, 0)
            far_onward(t)

            @pl.when(t >= 1)
            def _():
                far_home(t - 1)

            return 0

        lax.fori_loop(0, N_CHUNKS, down_range, 0)
        last = jnp.int32(N_CHUNKS - 1)

        for half in range(2):

            def own_chip(i, _):
                shared_down(i, half)
                if half == 0:

                    @pl.when(i == 0)
                    def _():
                        near_home(last)

                spread(half * (N_CHUNKS // 2) + i, chip)
                return 0

            lax.fori_loop(0, N_CHUNKS // 2, own_chip, 0)
        far_home(last)

        def own_sums(t, _):
            add_sib(t, chip)
            return 0

        lax.fori_loop(0, N_CHUNKS, own_sums, 0)

        for j in range(J_CHUNKS):
            cols = slice(j * jd, (j + 1) * jd)
            with jax.named_scope('home'):
                com_copy(jnp.int32(j)).wait_recv()
                dir_copy(jnp.int32(j)).wait_recv()
            routed = part[j, block(me), :] + (from_fin[0, j] + from_fin[1, j])
            shared_out = sh[j].astype(BF16).astype(F32)
            out_ref[:, cols] = (hid[:, cols].astype(F32) + shared_out + routed).astype(BF16)

        for j in range(J_CHUNKS):
            ji = jnp.int32(j)
            for c in range(chips):
                sib_copy(ji, c).wait_send()
            tr_copy(ji).wait_send()
            dir_copy(ji).wait_send()
            com_copy(ji).wait_send()

    pl.run_scoped(
        phase_one,
        pltpu.VMEM((experts * CAP, kd), BF16),
        pltpu.VMEM((experts * CAP, total), BF16),
        pltpu.VMEM((experts, CAP, ff), F32),
        pltpu.VMEM((experts, CAP, ff), F32),
        pltpu.VMEM((halves, rows, ff), F32),
        pltpu.VMEM((halves, rows, ff), F32),
        pltpu.VMEM((UP_SLOTS, 2, kd, ff), BF16),
    )
    pl.run_scoped(
        phase_two,
        pltpu.VMEM((N_CHUNKS, experts, CAP, nd), BF16),
        pltpu.VMEM((J_CHUNKS, total, jd), F32),
        pltpu.VMEM((slots, ff, nd), BF16),
    )


def routed_layer(n, *args):
    hidden, norm_gain, w_gate, w1_shared, w3_shared, w2_shared, w1_experts, w3_experts, w2_experts, topk_ids = args
    rows, width = hidden.shape
    experts, _, ff = w1_experts.shape
    total = n * rows
    chips = n // 2
    kd = width // K_CHUNKS
    jd = width // J_CHUNKS
    nd = width // N_CHUNKS
    halves = w1_shared.shape[1] // ff
    dma = pltpu.SemaphoreType.DMA
    vmem = pltpu.VMEM
    scratch = [
        vmem((rows, width), BF16),
        vmem((1, width), BF16),
        vmem(w_gate.shape[::-1], BF16),
        vmem(topk_ids.shape[::-1], jnp.int32),
        vmem((128, 128), F32),
        vmem((n, 16, 128), F32),
        vmem((total, 128), F32),
        vmem((total, 128), F32),
        vmem((K_CHUNKS, total, kd), BF16),
        vmem((experts, total, CAP), BF16),
        vmem((experts, total, 128), F32),
        vmem((experts, CAP, ff), BF16),
        vmem((halves, rows, ff), BF16),
        vmem((J_CHUNKS, rows, jd), F32),
        vmem((J_CHUNKS, chips, rows, jd), F32),
        vmem((J_CHUNKS, rows, jd), F32),
        vmem((2, J_CHUNKS, rows, jd), F32),
        vmem((experts // 2, ff, nd), BF16),
        dma((4,)),
        dma((n,)),
        dma((n,)),
        dma((K_CHUNKS, 7)),
        dma((K_CHUNKS, n)),
        dma((UP_SLOTS, 2)),
        dma((experts,)),
        dma((J_CHUNKS, chips)),
        dma((J_CHUNKS, chips)),
        dma((J_CHUNKS,)),
        dma((J_CHUNKS,)),
        dma((J_CHUNKS,)),
        dma((J_CHUNKS,)),
        dma((2, J_CHUNKS)),
    ]
    return pl.pallas_call(
        functools.partial(moe_kernel, n),
        out_shape=[jax.ShapeDtypeStruct((rows, width), BF16), jax.ShapeDtypeStruct((1, 1), jnp.int32)],
        in_specs=[pl.BlockSpec(memory_space=pl.ANY)] * 10,
        out_specs=[pl.BlockSpec(memory_space=pltpu.VMEM), pl.BlockSpec(memory_space=pltpu.SMEM)],
        scratch_shapes=scratch,
        compiler_params=pltpu.CompilerParams(collective_id=0, has_side_effects=True, vmem_limit_bytes=67043328),
        name='moe_layer',
    )(hidden, norm_gain.reshape(1, width), w_gate.T, *args[3:9], topk_ids.T)


def solution(mesh):
    n = mesh.shape['ep']
    tok_spec = P(('dp', 'ep'), None)
    expert_spec = P('ep', None, None)

    def local_fn(*args):
        out, over = routed_layer(n, *args)
        return lax.switch(over[0, 0], (lambda: out, lambda: dense_path(n, *args)))

    return jax.shard_map(local_fn, mesh=mesh, in_specs=(tok_spec, P(), P(), P(), P(), P(), expert_spec, expert_spec, expert_spec, tok_spec), out_specs=tok_spec, check_vma=False)
```

time: 257 us -> 87.2 us (0.34)
  matrix products: 170 us -> 0 us
  Pallas kernels: 0 us -> 83.2 us
  waiting for transfers between devices: 34.9 us -> 0 us
  blocking collectives: 28 us -> 0 us
  between operations: 13.6 us -> 0.58 us
  other arithmetic: 5.27 us -> 0 us
    dot_general x6 -> x0, matrix products: 170 us -> none  [the longest x1 52.7 us: routed_experts(): jnp.einsum('nd,edf->enf', rows_in, w1_experts, preferred_element_type=jnp...]
    pallas_call x0 -> x1, Pallas kernels: none -> 83.2 us  [routed_layer(): pl.pallas_call(functools.partial(moe_kernel, n), out_shape=[jax.ShapeDtyp...]
    reduce_scatter x1 -> x0, waiting for transfers between devices: 34.8 us -> none  [local_fn(): routed = lax.psum_scatter(part_sum, 'ep', scatter_dimension=0, tiled=True)]
    all_gather x2 -> x0, blocking collectives: 28 us -> none  [the longest x1 14.9 us: local_fn(): all_wts = lax.all_gather(gate_wts, 'ep', axis=0, tiled=True)]
    gather x5 -> x0, local copies, waits for them, and re-layouts: 4.47 us -> none  [router_weights(): return ROUTE_SCALE * jnp.take_along_axis(gate_probs, topk_ids, axis=1)]
    convert_element_type x2 -> x0, other arithmetic: 2.64 us -> none  [the longest x1 1.9 us: rms_norm(): (rows_f * inv_rms * norm_gain.astype(jnp.float32)).astype(jnp.bfloat16)]
  transfers between devices with their start and end apart: 2 -> 0, of which waited for: 1 -> 0; matrix products, arithmetic and copies ran while one was open for 5% -> 0% of each run, Pallas kernels for 0% -> 0%
where the time goes in v2:
time: 87.2 us; the launch traced here: 87 us
  Pallas kernels  83.2 us (95%)
  local copies, waits for them, and re-layouts  3.06 us (4%)
    pallas_call x1, Pallas kernels, routed_layer(): pl.pallas_call(functools.partial(moe_kernel, n), out_shape=[jax.ShapeDtyp...  83.2 us
    unnamed x1, local copies, waits for them, and re-layouts  1.77 us

profile of v2, /device:TPU:81, one launch (start us, length us, event | category | flops | bytes accessed | tf_op | source)
XLA Modules:
  0.0 87.0 jit_solution(12549981066756448790)
XLA Ops:
  0.0 1.3 %reshape.30.gain_hbm = bf16[1,2048]{1,0:T(2,128)(2,1)} reshape(bf16[2048]{0:T(1024)(128)(2,1)} %param.15) | data formatting | bytes 8192 | tf_op jit(solution)/shard_map/reshape | solution.py:594
  1.3 83.2 %moe_layer.1 = (bf16[96,2048]{1,0:T(8,128)(2,1)}, s32[1,1]{1,0:T(1,128)}) custom-call(bf16[96,2048]{1,0:T(8,128)(2,1)} %hid_hbm.1, bf16[1,2048]{1,0:T(2,128)(2,1)} %reshape.30.gain_hbm, bf16[64,2048]{1,0:T(8,128)(2,1)} %bitcast.77, bf16[2048,2816]{1,0:T(8,128)(2,1)} %w1s.1, bf16[2048,2816]{1,0:T(8,128)(2,1)} %w3s.1, bf16[2816,2048]{1,0:T(8,128)(2,1)} %w2s.1, ...), custom_call_target="tpu_custom_call" | custom-call | tf_op jit(solution)/shard_map/moe_layer/pallas_call | solution.py:586
  85.0 0.2 conditional.1
  85.3 1.8 %copy.40 = bf16[96,2048]{1,0:T(8,128)(2,1)} copy(bf16[96,2048]{1,0:T(8,128)(2,1)} %get-tuple-element.90) | data formatting | bytes 786432

commit v3 on v2

--- a/solution.py
+++ b/solution.py
@@ -14,6 +14,7 @@
 J_CHUNKS = 8
 N_CHUNKS = 4
 UP_SLOTS = 7
+EARLY = 4
 
 F32 = jnp.float32
 BF16 = jnp.bfloat16
@@ -63,10 +64,10 @@
 def moe_kernel(
     n, hid_hbm, gain_hbm, wg_hbm, w1s, w3s, w2s, w1e, w3e, w2e, ids_hbm,
     out_ref, over_ref,
-    hid, gain, wg, ids, tile, info, wmap, rank, x_all, ssel, wb, inner, sinner, sh,
-    from_sib, from_tr, from_fin, bbuf,
-    in_sem, info_send, info_recv, ag_send, ag_recv, a_sem, b_sem,
-    sib_send, sib_recv, tr_send, tr_recv, dir_send, com_send, fin_recv,
+    hid, gain, wg, ids, tile, info, wmap, rank, x_all, ssel, wb, inner, sacc1, sacc3, sinner, sh,
+    from_sib, from_tr, from_fin, bbuf, bbuf_hi, obuf, over,
+    in_sem, info_send, info_recv, ag_send, ag_recv, a_sem, s_sem, b_sem,
+    sib_send, sib_recv, tr_send, tr_recv, dir_send, com_send, fin_recv, out_sem, over_sem,
 ):
     rows, width = hid.shape
     experts, _, ff = w1e.shape
@@ -80,6 +81,8 @@
     n_shared = K_CHUNKS * halves
     n_up = K_CHUNKS * experts
     slots = experts // 2
+    n_set = K_CHUNKS * slots
+    late = n_shared - EARLY
 
     me = lax.axis_index('ep')
     chip, core = me // 2, lax.rem(me, 2)
@@ -120,53 +123,81 @@
             src_ref=src, dst_ref=dst, send_sem=send, recv_sem=recv, device_id={'ep': to}, device_id_type=pl.DeviceIdType.MESH
         )
 
-    def phase_one(xg, gsel, acc1, acc3, sacc1, sacc3, abuf):
+    def shared_src(s):
+        k, h = s // halves, lax.rem(s, halves)
+        at = (pl.ds(pl.multiple_of(k * kd, 128), kd), pl.ds(pl.multiple_of(h * ff, 128), ff))
+        return w1s.at[at], w3s.at[at]
+
+    def two_products(buf, x, slot, put):
+        cut = ff // 256 * 256
+        put(0, slice(0, cut), jnp.dot(x, buf[slot, 0, :, 0:cut], preferred_element_type=F32))
+        put(1, slice(0, cut), jnp.dot(x, buf[slot, 1, :, 0:cut], preferred_element_type=F32))
+        if cut < ff:
+            rest = jnp.concatenate([buf[slot, 0, :, cut:ff], buf[slot, 1, :, cut:ff]], axis=1)
+            d = jnp.dot(x, rest, preferred_element_type=F32)
+            put(0, slice(cut, ff), d[:, : ff - cut])
+            put(1, slice(cut, ff), d[:, ff - cut :])
+
+    def shared_product(s, buf, slot):
+        k, h = s // halves, lax.rem(s, halves)
+
+        def put(i, cols, d):
+            acc = (sacc1, sacc3)[i]
+            acc[h, :, cols] = d + jnp.where(k == 0, 0.0, acc[h, :, cols])
+
+        two_products(buf, x_all[k, block(me), :], slot, put)
+
+    def late_copies(i, sbuf):
+        return [
+            pltpu.make_async_copy(src, sbuf.at[i, m], s_sem.at[i, m])
+            for m, src in enumerate(shared_src(jnp.int32(EARLY) + i))
+        ]
+
+    def late_shared(i, sbuf):
+        for copy in late_copies(i, sbuf):
+            copy.start()
+
+    over_copy = pltpu.make_async_copy(over, over_ref, over_sem)
+
+    def phase_one(xg, gsel, acc1, acc3, abuf):
         def up_pair(pair, slot):
             return [pltpu.make_async_copy(src, abuf.at[slot, i], a_sem.at[slot, i]) for i, src in enumerate(pair)]
 
         def up_shared(s):
-            k, h = s // halves, lax.rem(s, halves)
-            at = (pl.ds(pl.multiple_of(k * kd, 128), kd), pl.ds(pl.multiple_of(h * ff, 128), ff))
-            return up_pair((w1s.at[at], w3s.at[at]), lax.rem(s, UP_SLOTS))
+            return up_pair(shared_src(s), lax.rem(s, UP_SLOTS))
 
         def up_routed(q):
-            k, e = q // experts, lax.rem(q, experts)
+            k, e = lax.rem(q // slots, K_CHUNKS), q // n_set * slots + lax.rem(q, slots)
             at = (e, pl.ds(pl.multiple_of(k * kd, 128), kd))
-            return up_pair((w1e.at[at], w3e.at[at]), lax.rem(q + n_shared, UP_SLOTS))
+            return up_pair((w1e.at[at], w3e.at[at]), lax.rem(q + EARLY, UP_SLOTS))
 
         def start_up(s):
-            if isinstance(s, int):
-                if s < n_shared:
-                    for copy in up_shared(jnp.int32(s)):
-                        copy.start()
-                elif s < n_shared + n_up:
-                    for copy in up_routed(jnp.int32(s - n_shared)):
-                        copy.start()
-                return
-
-            @pl.when(s < n_shared)
+            @pl.when(s < EARLY)
             def _():
                 for copy in up_shared(s):
                     copy.start()
 
-            @pl.when((s >= n_shared) & (s < n_shared + n_up))
+            @pl.when((s >= EARLY) & (s < EARLY + n_up))
             def _():
-                for copy in up_routed(s - n_shared):
+                for copy in up_routed(s - EARLY):
                     copy.start()
 
         with jax.named_scope('small_in'):
             for copy in small:
                 copy.wait()
         for s in range(UP_SLOTS):
-            start_up(s)
+            start_up(jnp.int32(s))
         for e in range(experts // 2):
             down_routed(0, e, bbuf, e, e).start()
+        for e in range(experts // 2):
+            down_routed(0, slots + e, bbuf_hi, e, slots + e).start()
         with jax.named_scope('norm'):
             rows_f = hid[...].astype(F32)
             inv_rms = lax.rsqrt(jnp.mean(rows_f * rows_f, axis=-1, keepdims=True) + NORM_EPS)
-            for k in range(K_CHUNKS):
-                cols = slice(k * kd, (k + 1) * kd)
-                x_all[k, block(me), :] = (rows_f[:, cols] * inv_rms * gain[:, cols].astype(F32)).astype(BF16)
+            for i in range(width // 128):
+                piece = rows_f[:, i * 128 : (i + 1) * 128] * inv_rms * gain[i : i + 1, :].astype(F32)
+                off = i * 128 % kd
+                x_all[i * 128 // kd, block(me), off : off + 128] = piece.astype(BF16)
         with jax.named_scope('barrier'):
             pl.semaphore_wait(barrier, n - 1)
 
@@ -198,7 +229,6 @@
                 rows_copy(k, dev(chip + i, 1 - core), 0, sib).wait_recv()
 
         send_own(0)
-        send_own(1)
 
         logits = jnp.concatenate([x_all[k, block(me), :] for k in range(K_CHUNKS)], axis=1)
         logits = lax.dot_general(logits, wg[...], (((1,), (1,)), ((), ())), preferred_element_type=F32)
@@ -223,133 +253,134 @@
         def info_copy(i, b, to):
             return remote(info.at[b], info.at[b], info_send.at[i], info_recv.at[b], to)
 
+        for i in range(1, n):
+            info_copy(i, me, lax.rem(me + i, n)).start()
+        send_own(1)
+
         def shared_step(s, _):
-            k, h = s // halves, lax.rem(s, halves)
             for copy in up_shared(s):
                 copy.wait()
-            slot = lax.rem(s, UP_SLOTS)
-            x = x_all[k, block(me), :]
-            for i, acc in enumerate((sacc1, sacc3)):
-                d = jnp.dot(x, abuf[slot, i], preferred_element_type=F32)
-                acc[h] = d + jnp.where(k == 0, 0.0, acc[h])
-
+            shared_product(s, abuf, lax.rem(s, UP_SLOTS))
             start_up(s + UP_SLOTS)
-
-            @pl.when(s == 0)
+            return 0
+
+        def shared_steps(first_s, last_s):
+            with jax.named_scope('shared_up'):
+                lax.fori_loop(first_s, last_s, shared_step, 0)
+
+        def tables():
+            for i in range(1, n):
+                b = lax.rem(me + i, n)
+                info_copy(i, b, b).wait_recv()
+            info_cols = info[...].reshape(n * 16, 128).T
+            first = (me * experts).astype(F32)
+            all_experts = float(n * experts)
+            lane_f = lax.broadcasted_iota(jnp.int32, (rows, 128), 1).astype(F32)
+            lower = lax.broadcasted_iota(jnp.int32, (rows, rows), 0) > lax.broadcasted_iota(jnp.int32, (rows, rows), 1)
+            lower = jnp.where(lower, 1.0, 0.0).astype(BF16)
+            seen = jnp.zeros((1, 128), F32)
+            for b in range(n):
+                wm = jnp.zeros((rows, 128), F32)
+                hit_any = jnp.zeros((rows, 128), F32)
+                for i in range(top_k):
+                    wt = info_cols[0:rows, 16 * b + i : 16 * b + i + 1]
+                    at = info_cols[0:rows, 16 * b + 8 + i : 16 * b + 9 + i] - first
+                    at = jnp.where(at < 0, at + all_experts, at)
+                    hit = lane_f == at
+                    wm = jnp.where(hit, wt, wm)
+                    hit_any = jnp.where(hit, 1.0, hit_any)
+                before = jnp.dot(lower, hit_any.astype(BF16), preferred_element_type=F32) + seen
+                wmap[b * rows : (b + 1) * rows, :] = wm
+                rank[b * rows : (b + 1) * rows, :] = jnp.where(hit_any > 0, before, -1.0)
+                seen = seen + jnp.sum(hit_any, axis=0, keepdims=True)
+            over[0, 0] = (jnp.max(seen) > CAP).astype(jnp.int32)
+            over_copy.start()
+            rank_rows = rank[...].T
+            place = lax.broadcasted_iota(jnp.int32, (CAP, total), 0).astype(F32)
+            for e in range(experts):
+                hit = place == jnp.broadcast_to(rank_rows[e : e + 1, :], (CAP, total))
+                gsel[e * CAP : (e + 1) * CAP, :] = jnp.where(hit, 1.0, 0.0).astype(BF16)
+
+        shared_steps(0, EARLY)
+        with jax.named_scope('near0'):
+            forward_near(jnp.int32(0))
+            send_own(jnp.int32(2))
+        with jax.named_scope('info'):
+            tables()
+        with jax.named_scope('near1'):
+            forward_near(jnp.int32(1))
+            send_own(jnp.int32(3))
+        with jax.named_scope('select'):
+            place_lane = lax.broadcasted_iota(jnp.int32, (total, CAP), 1).astype(F32)
+            for e in range(experts):
+                hit = place_lane == jnp.broadcast_to(rank[:, e : e + 1], (total, CAP))
+                ssel[e] = jnp.where(hit, 1.0, 0.0).astype(BF16)
+                wb[e] = jnp.broadcast_to(wmap[:, e : e + 1], (total, 128))
+        with jax.named_scope('far0'):
+            forward_far(jnp.int32(0))
+
+        def up_chunk(kk, _):
+            k, base = lax.rem(kk, K_CHUNKS), kk // K_CHUNKS * slots
+
+            @pl.when(kk < K_CHUNKS)
             def _():
-                for i in range(1, n):
-                    info_copy(i, me, lax.rem(me + i, n)).start()
-
-            @pl.when(s == 3)
-            def _():
-                forward_near(jnp.int32(0))
-                send_own(jnp.int32(2))
-
-            @pl.when(s == 6)
-            def _():
-                forward_near(jnp.int32(1))
-                send_own(jnp.int32(3))
+                with jax.named_scope('wait_rows'):
+                    wait_sib_rows(k)
+
+            with jax.named_scope('gather'):
+                span = pl.ds(pl.multiple_of(base * CAP, CAP), slots * CAP)
+                xg[...] = jnp.dot(gsel[span, :], x_all[k], preferred_element_type=F32).astype(BF16)
+
+            def up_step(g, _):
+                for u in range(2):
+                    for copy in up_routed(kk * slots + g * 2 + u):
+                        copy.wait()
+                for u in range(2):
+                    i_e = g * 2 + u
+
+                    def put(i, cols, d):
+                        acc = (acc1, acc3)[i]
+                        acc[i_e, :, cols] = d + jnp.where(k == 0, 0.0, acc[i_e, :, cols])
+
+                    two_products(
+                        abuf,
+                        xg[pl.ds(pl.multiple_of(i_e * CAP, CAP), CAP), :],
+                        lax.rem(kk * slots + i_e + EARLY, UP_SLOTS),
+                        put,
+                    )
+                for u in range(2):
+                    start_up(kk * slots + g * 2 + u + EARLY + UP_SLOTS)
+
+                @pl.when((g == 1) & (kk + 1 < K_CHUNKS))
+                def _():
+                    forward_far(kk + 1)
+
+                @pl.when((g == 0) & (kk + 2 < K_CHUNKS))
+                def _():
+                    forward_near(kk + 2)
+
+                @pl.when(k == K_CHUNKS - 1)
+                def _():
+                    for u in range(2):
+                        i_e = g * 2 + u
+                        inner[base + i_e] = (jax.nn.silu(acc1[i_e]) * acc3[i_e]).astype(BF16)
+
+                return 0
+
+            with jax.named_scope('up_steps'):
+                lax.fori_loop(0, slots // 2, up_step, 0)
 
             return 0
 
-        with jax.named_scope('shared_up'):
-            lax.fori_loop(0, n_shared, shared_step, 0)
-
-        for i in range(1, n):
-            b = lax.rem(me + i, n)
-            info_copy(i, b, b).wait_recv()
-        info_cols = info[...].reshape(n * 16, 128).T
-        first = (me * experts).astype(F32)
-        all_experts = float(n * experts)
-        lane_f = lax.broadcasted_iota(jnp.int32, (rows, 128), 1).astype(F32)
-        lower = lax.broadcasted_iota(jnp.int32, (rows, rows), 0) > lax.broadcasted_iota(jnp.int32, (rows, rows), 1)
-        lower = jnp.where(lower, 1.0, 0.0).astype(BF16)
-        seen = jnp.zeros((1, 128), F32)
-        for b in range(n):
-            wm = jnp.zeros((rows, 128), F32)
-            hit_any = jnp.zeros((rows, 128), F32)
-            for i in range(top_k):
-                wt = info_cols[0:rows, 16 * b + i : 16 * b + i + 1]
-                at = info_cols[0:rows, 16 * b + 8 + i : 16 * b + 9 + i] - first
-                at = jnp.where(at < 0, at + all_experts, at)
-                hit = lane_f == at
-                wm = jnp.where(hit, wt, wm)
-                hit_any = jnp.where(hit, 1.0, hit_any)
-            before = jnp.dot(lower, hit_any.astype(BF16), preferred_element_type=F32) + seen
-            wmap[b * rows : (b + 1) * rows, :] = wm
-            rank[b * rows : (b + 1) * rows, :] = jnp.where(hit_any > 0, before, -1.0)
-            seen = seen + jnp.sum(hit_any, axis=0, keepdims=True)
-        over_ref[0, 0] = (jnp.max(seen) > CAP).astype(jnp.int32)
-        rank_rows = rank[...].T
-        place = lax.broadcasted_iota(jnp.int32, (CAP, total), 0).astype(F32)
-        for e in range(experts):
-            hit = place == jnp.broadcast_to(rank_rows[e : e + 1, :], (CAP, total))
-            gsel[e * CAP : (e + 1) * CAP, :] = jnp.where(hit, 1.0, 0.0).astype(BF16)
-
-        forward_far(jnp.int32(0))
-
-        def up_chunk(k, _):
-            with jax.named_scope('wait_rows'):
-                wait_sib_rows(k)
-            for half in range(2):
-                span = slice(half * experts * CAP // 2, (half + 1) * experts * CAP // 2)
-                xg[span, :] = jnp.dot(gsel[span, :], x_all[k], preferred_element_type=F32).astype(BF16)
-
-            def up_step(e, _):
-                q = k * experts + e
-                for copy in up_routed(q):
-                    copy.wait()
-                slot = lax.rem(q + n_shared, UP_SLOTS)
-                x = xg[pl.ds(pl.multiple_of(e * CAP, CAP), CAP), :]
-                for i, acc in enumerate((acc1, acc3)):
-                    d = jnp.dot(x, abuf[slot, i], preferred_element_type=F32)
-                    acc[e] = d + jnp.where(k == 0, 0.0, acc[e])
-
-                start_up(q + n_shared + UP_SLOTS)
-
-                for i in range(experts):
-
-                    @pl.when((k == 1) & (e == i))
-                    def _():
-                        slots = lax.broadcasted_iota(jnp.int32, (total, CAP), 1).astype(F32)
-                        hit = slots == jnp.broadcast_to(rank[:, i : i + 1], (total, CAP))
-                        ssel[i] = jnp.where(hit, 1.0, 0.0).astype(BF16)
-                        wb[i] = jnp.broadcast_to(wmap[:, i : i + 1], (total, 128))
-
-                @pl.when((e == 3) & (k + 1 < K_CHUNKS))
-                def _():
-                    forward_far(k + 1)
-
-                @pl.when((e == 3) & (k + 2 < K_CHUNKS))
-                def _():
-                    forward_near(k + 2)
-
-                return 0
-
-            with jax.named_scope('up_steps'):
-                lax.fori_loop(0, experts, up_step, 0)
-
-            return 0
-
-        lax.fori_loop(0, K_CHUNKS, up_chunk, 0)
-
-        def activate(e, _):
-            inner[e] = (jax.nn.silu(acc1[e]) * acc3[e]).astype(BF16)
-            return 0
-
-        with jax.named_scope('act'):
-            lax.fori_loop(0, experts, activate, 0)
-        for h in range(halves):
-            sinner[h] = (jax.nn.silu(sacc1[h]) * sacc3[h]).astype(BF16)
+        lax.fori_loop(0, 2 * K_CHUNKS, up_chunk, 0)
         for i in range(1, n):
             info_copy(i, me, lax.rem(me + i, n)).wait_send()
         for k in range(K_CHUNKS):
             for lane_i in range(7):
                 rows_copy(jnp.int32(k), me, lane_i, sib).wait_send()
 
-    def phase_two(ebuf, part, bbuf_hi):
-        for e in range(slots):
-            down_routed(0, slots + e, bbuf_hi, e, slots + e).start()
+    def phase_two(ebuf, part, sbuf):
+        late_shared(0, sbuf)
         def sib_copy(j, c):
             return remote(
                 part.at[j, block(c * 2 + (1 - core))], from_sib.at[j, c], sib_send.at[j, c], sib_recv.at[j, c], sib
@@ -372,30 +403,26 @@
 
         def products(t, half):
             buf = (bbuf, bbuf_hi)[half]
-
-            def down_step(g, _):
-                for u in range(2):
-                    slot = g * 2 + u
+            with jax.named_scope('products'):
+                for slot in range(slots):
                     e = half * slots + slot
                     down_routed(t, e, buf, slot, e).wait()
+                for slot in range(slots):
+                    e = half * slots + slot
                     d = jnp.dot(inner[e], buf[slot], preferred_element_type=F32)
                     ebuf[t, e] = d.astype(BF16)
-                for u in range(2):
-                    slot = g * 2 + u
-                    e = half * slots + slot
-
-                    @pl.when(t + 1 < N_CHUNKS)
-                    def _():
+
+                @pl.when(t + 1 < N_CHUNKS)
+                def _():
+                    for slot in range(slots):
+                        e = half * slots + slot
                         down_routed(t + 1, e, buf, slot, e).start()
 
-                    @pl.when(t + 1 == N_CHUNKS)
-                    def _():
+                @pl.when(t + 1 == N_CHUNKS)
+                def _():
+                    for slot in range(slots):
+                        e = half * slots + slot
                         down_shared(e, buf, slot, e).start()
-
-                return 0
-
-            with jax.named_scope('products'):
-                lax.fori_loop(0, slots // 2, down_step, 0)
 
         def spread(t, c):
             span = pl.ds(pl.multiple_of(c * 2 * rows, 32), 2 * rows)
@@ -464,12 +491,23 @@
 
             products(t, 1)
 
-            def three(i, _):
-                spread(t, lax.rem(chip + 2 - i + 3 * (i // 2), chips))
+            spread(t, chip_far)
+
+            def near(i, _):
+                spread(t, lax.rem(chip + 1 + 2 * i, chips))
                 return 0
 
-            lax.fori_loop(0, 3, three, 0)
+            lax.fori_loop(0, 2, near, 0)
             far_onward(t)
+
+            @pl.when(t + 1 < late)
+            def _():
+                late_shared(t + 1, sbuf)
+
+            with jax.named_scope('late_shared'):
+                for copy in late_copies(t, sbuf):
+                    copy.wait()
+                shared_product(EARLY + t, sbuf, t)
 
             @pl.when(t >= 1)
             def _():
@@ -479,6 +517,8 @@
 
         lax.fori_loop(0, N_CHUNKS, down_range, 0)
         last = jnp.int32(N_CHUNKS - 1)
+        for h in range(halves):
+            sinner[h] = (jax.nn.silu(sacc1[h]) * sacc3[h]).astype(BF16)
 
         for half in range(2):
 
@@ -509,31 +549,35 @@
                 dir_copy(jnp.int32(j)).wait_recv()
             routed = part[j, block(me), :] + (from_fin[0, j] + from_fin[1, j])
             shared_out = sh[j].astype(BF16).astype(F32)
-            out_ref[:, cols] = (hid[:, cols].astype(F32) + shared_out + routed).astype(BF16)
-
-        for j in range(J_CHUNKS):
-            ji = jnp.int32(j)
-            for c in range(chips):
-                sib_copy(ji, c).wait_send()
-            tr_copy(ji).wait_send()
-            dir_copy(ji).wait_send()
-            com_copy(ji).wait_send()
+            obuf[:, cols] = (hid[:, cols].astype(F32) + shared_out + routed).astype(BF16)
+            pltpu.make_async_copy(obuf.at[:, cols], out_ref.at[:, cols], out_sem.at[j]).start()
+
+        with jax.named_scope('sent'):
+            over_copy.wait()
+            for j in range(J_CHUNKS):
+                ji = jnp.int32(j)
+                for c in range(chips):
+                    sib_copy(ji, c).wait_send()
+                tr_copy(ji).wait_send()
+                dir_copy(ji).wait_send()
+                com_copy(ji).wait_send()
+            for j in range(J_CHUNKS):
+                cols = slice(j * jd, (j + 1) * jd)
+                pltpu.make_async_copy(obuf.at[:, cols], out_ref.at[:, cols], out_sem.at[j]).wait()
 
     pl.run_scoped(
         phase_one,
-        pltpu.VMEM((experts * CAP, kd), BF16),
+        pltpu.VMEM((experts // 2 * CAP, kd), BF16),
         pltpu.VMEM((experts * CAP, total), BF16),
-        pltpu.VMEM((experts, CAP, ff), F32),
-        pltpu.VMEM((experts, CAP, ff), F32),
-        pltpu.VMEM((halves, rows, ff), F32),
-        pltpu.VMEM((halves, rows, ff), F32),
+        pltpu.VMEM((experts // 2, CAP, ff), F32),
+        pltpu.VMEM((experts // 2, CAP, ff), F32),
         pltpu.VMEM((UP_SLOTS, 2, kd, ff), BF16),
     )
     pl.run_scoped(
         phase_two,
         pltpu.VMEM((N_CHUNKS, experts, CAP, nd), BF16),
         pltpu.VMEM((J_CHUNKS, total, jd), F32),
-        pltpu.VMEM((slots, ff, nd), BF16),
+        pltpu.VMEM((late, 2, kd, ff), BF16),
     )
 
 
@@ -551,7 +595,7 @@
     vmem = pltpu.VMEM
     scratch = [
         vmem((rows, width), BF16),
-        vmem((1, width), BF16),
+        vmem((width // 128, 128), BF16),
         vmem(w_gate.shape[::-1], BF16),
         vmem(topk_ids.shape[::-1], jnp.int32),
         vmem((128, 128), F32),
@@ -562,18 +606,24 @@
         vmem((experts, total, CAP), BF16),
         vmem((experts, total, 128), F32),
         vmem((experts, CAP, ff), BF16),
+        vmem((halves, rows, ff), F32),
+        vmem((halves, rows, ff), F32),
         vmem((halves, rows, ff), BF16),
         vmem((J_CHUNKS, rows, jd), F32),
         vmem((J_CHUNKS, chips, rows, jd), F32),
         vmem((J_CHUNKS, rows, jd), F32),
         vmem((2, J_CHUNKS, rows, jd), F32),
         vmem((experts // 2, ff, nd), BF16),
+        vmem((experts // 2, ff, nd), BF16),
+        vmem((rows, width), BF16),
+        pltpu.SMEM((1, 1), jnp.int32),
         dma((4,)),
         dma((n,)),
         dma((n,)),
         dma((K_CHUNKS, 7)),
         dma((K_CHUNKS, n)),
         dma((UP_SLOTS, 2)),
+        dma((K_CHUNKS * halves - EARLY, 2)),
         dma((experts,)),
         dma((J_CHUNKS, chips)),
         dma((J_CHUNKS, chips)),
@@ -582,16 +632,18 @@
         dma((J_CHUNKS,)),
         dma((J_CHUNKS,)),
         dma((2, J_CHUNKS)),
+        dma((J_CHUNKS,)),
+        dma(()),
     ]
     return pl.pallas_call(
         functools.partial(moe_kernel, n),
         out_shape=[jax.ShapeDtypeStruct((rows, width), BF16), jax.ShapeDtypeStruct((1, 1), jnp.int32)],
         in_specs=[pl.BlockSpec(memory_space=pl.ANY)] * 10,
-        out_specs=[pl.BlockSpec(memory_space=pltpu.VMEM), pl.BlockSpec(memory_space=pltpu.SMEM)],
+        out_specs=[pl.BlockSpec(memory_space=pl.ANY), pl.BlockSpec(memory_space=pl.ANY)],
         scratch_shapes=scratch,
         compiler_params=pltpu.CompilerParams(collective_id=0, has_side_effects=True, vmem_limit_bytes=67043328),
         name='moe_layer',
-    )(hidden, norm_gain.reshape(1, width), w_gate.T, *args[3:9], topk_ids.T)
+    )(hidden, norm_gain.reshape(-1, 128), w_gate.T, *args[3:9], topk_ids.T)
 
 
 def solution(mesh):

time: 87.2 us -> 78.4 us (0.90)
  Pallas kernels: 83.2 us -> 75.7 us
  local copies, waits for them, and re-layouts: 3.06 us -> 1.77 us
    pallas_call x1, Pallas kernels: 83.2 us -> 75.7 us  [routed_layer(): pl.pallas_call(functools.partial(moe_kernel, n), out_shape=[jax.ShapeDtyp...]
    reshape x1 -> x0, local copies, waits for them, and re-layouts: 1.29 us -> none  [routed_layer(): norm_gain.reshape(1, width)]
where the time goes in v3:
time: 78.4 us; the launch traced here: 78.3 us
  Pallas kernels  75.7 us (97%)
  local copies, waits for them, and re-layouts  1.77 us (2%)
    pallas_call x1, Pallas kernels, routed_layer(): pl.pallas_call(functools.partial(moe_kernel, n), out_shape=[jax.ShapeDtyp...  75.7 us
    unnamed x1, local copies, waits for them, and re-layouts  1.77 us

profile of v3, /device:TPU:81, one launch (start us, length us, event | category | flops | bytes accessed | tf_op | source)
XLA Modules:
  0.0 78.3 jit_solution(4509509486738613411)
XLA Ops:
  0.0 75.7 %moe_layer.1 = (bf16[96,2048]{1,0:T(8,128)(2,1)}, s32[1,1]{1,0:T(1,128)}) custom-call(bf16[96,2048]{1,0:T(8,128)(2,1)} %hid_hbm.1, bf16[16,128]{1,0:T(8,128)(2,1)} %bitcast.81, bf16[64,2048]{1,0:T(8,128)(2,1)} %bitcast.78, bf16[2048,2816]{1,0:T(8,128)(2,1)} %w1s.1, bf16[2048,2816]{1,0:T(8,128)(2,1)} %w3s.1, bf16[2816,2048]{1,0:T(8,128)(2,1)} %w2s.1, ...), custom_call_target="tpu_custom_call" | custom-call | tf_op jit(solution)/shard_map/moe_layer/pallas_call | solution.py:638
  76.3 0.2 conditional.1
  76.5 1.8 %copy.40 = bf16[96,2048]{1,0:T(8,128)(2,1)} copy(bf16[96,2048]{1,0:T(8,128)(2,1)} %get-tuple-element.90) | data formatting | bytes 786432

commit v4 on v3

--- a/solution.py
+++ b/solution.py
@@ -14,7 +14,7 @@
 J_CHUNKS = 8
 N_CHUNKS = 4
 UP_SLOTS = 7
-EARLY = 4
+LATE_SLOTS = 4
 
 F32 = jnp.float32
 BF16 = jnp.bfloat16
@@ -64,8 +64,8 @@
 def moe_kernel(
     n, hid_hbm, gain_hbm, wg_hbm, w1s, w3s, w2s, w1e, w3e, w2e, ids_hbm,
     out_ref, over_ref,
-    hid, gain, wg, ids, tile, info, wmap, rank, x_all, ssel, wb, inner, sacc1, sacc3, sinner, sh,
-    from_sib, from_tr, from_fin, bbuf, bbuf_hi, obuf, over,
+    hid, gain, wg, ids, tile, info, wmap, rank, x_all, ssel, wb, inner,
+    from_sib, from_tr, from_fin, bbuf, bbuf_hi, over,
     in_sem, info_send, info_recv, ag_send, ag_recv, a_sem, s_sem, b_sem,
     sib_send, sib_recv, tr_send, tr_recv, dir_send, com_send, fin_recv, out_sem, over_sem,
 ):
@@ -81,8 +81,7 @@
     n_shared = K_CHUNKS * halves
     n_up = K_CHUNKS * experts
     slots = experts // 2
-    n_set = K_CHUNKS * slots
-    late = n_shared - EARLY
+    turn = n_shared // N_CHUNKS
 
     me = lax.axis_index('ep')
     chip, core = me // 2, lax.rem(me, 2)
@@ -138,48 +137,21 @@
             put(0, slice(cut, ff), d[:, : ff - cut])
             put(1, slice(cut, ff), d[:, ff - cut :])
 
-    def shared_product(s, buf, slot):
-        k, h = s // halves, lax.rem(s, halves)
-
-        def put(i, cols, d):
-            acc = (sacc1, sacc3)[i]
-            acc[h, :, cols] = d + jnp.where(k == 0, 0.0, acc[h, :, cols])
-
-        two_products(buf, x_all[k, block(me), :], slot, put)
-
-    def late_copies(i, sbuf):
-        return [
-            pltpu.make_async_copy(src, sbuf.at[i, m], s_sem.at[i, m])
-            for m, src in enumerate(shared_src(jnp.int32(EARLY) + i))
-        ]
-
-    def late_shared(i, sbuf):
-        for copy in late_copies(i, sbuf):
-            copy.start()
-
     over_copy = pltpu.make_async_copy(over, over_ref, over_sem)
 
     def phase_one(xg, gsel, acc1, acc3, abuf):
         def up_pair(pair, slot):
             return [pltpu.make_async_copy(src, abuf.at[slot, i], a_sem.at[slot, i]) for i, src in enumerate(pair)]
 
-        def up_shared(s):
-            return up_pair(shared_src(s), lax.rem(s, UP_SLOTS))
-
         def up_routed(q):
-            k, e = lax.rem(q // slots, K_CHUNKS), q // n_set * slots + lax.rem(q, slots)
+            k, e = q // experts, lax.rem(q, experts)
             at = (e, pl.ds(pl.multiple_of(k * kd, 128), kd))
-            return up_pair((w1e.at[at], w3e.at[at]), lax.rem(q + EARLY, UP_SLOTS))
-
-        def start_up(s):
-            @pl.when(s < EARLY)
+            return up_pair((w1e.at[at], w3e.at[at]), lax.rem(q, UP_SLOTS))
+
+        def start_up(q):
+            @pl.when(q < n_up)
             def _():
-                for copy in up_shared(s):
-                    copy.start()
-
-            @pl.when((s >= EARLY) & (s < EARLY + n_up))
-            def _():
-                for copy in up_routed(s - EARLY):
+                for copy in up_routed(q):
                     copy.start()
 
         with jax.named_scope('small_in'):
@@ -256,17 +228,6 @@
         for i in range(1, n):
             info_copy(i, me, lax.rem(me + i, n)).start()
         send_own(1)
-
-        def shared_step(s, _):
-            for copy in up_shared(s):
-                copy.wait()
-            shared_product(s, abuf, lax.rem(s, UP_SLOTS))
-            start_up(s + UP_SLOTS)
-            return 0
-
-        def shared_steps(first_s, last_s):
-            with jax.named_scope('shared_up'):
-                lax.fori_loop(first_s, last_s, shared_step, 0)
 
         def tables():
             for i in range(1, n):
@@ -301,7 +262,6 @@
                 hit = place == jnp.broadcast_to(rank_rows[e : e + 1, :], (CAP, total))
                 gsel[e * CAP : (e + 1) * CAP, :] = jnp.where(hit, 1.0, 0.0).astype(BF16)
 
-        shared_steps(0, EARLY)
         with jax.named_scope('near0'):
             forward_near(jnp.int32(0))
             send_own(jnp.int32(2))
@@ -319,68 +279,98 @@
         with jax.named_scope('far0'):
             forward_far(jnp.int32(0))
 
-        def up_chunk(kk, _):
-            k, base = lax.rem(kk, K_CHUNKS), kk // K_CHUNKS * slots
-
-            @pl.when(kk < K_CHUNKS)
-            def _():
-                with jax.named_scope('wait_rows'):
-                    wait_sib_rows(k)
-
+        def up_chunk(k, last):
+            with jax.named_scope('wait_rows'):
+                wait_sib_rows(k)
             with jax.named_scope('gather'):
-                span = pl.ds(pl.multiple_of(base * CAP, CAP), slots * CAP)
-                xg[...] = jnp.dot(gsel[span, :], x_all[k], preferred_element_type=F32).astype(BF16)
+                for half in range(2):
+                    span = slice(half * experts * CAP // 2, (half + 1) * experts * CAP // 2)
+                    xg[span, :] = jnp.dot(gsel[span, :], x_all[k], preferred_element_type=F32).astype(BF16)
 
             def up_step(g, _):
                 for u in range(2):
-                    for copy in up_routed(kk * slots + g * 2 + u):
+                    for copy in up_routed(k * experts + g * 2 + u):
                         copy.wait()
                 for u in range(2):
-                    i_e = g * 2 + u
+                    e = g * 2 + u
+                    q = k * experts + e
 
                     def put(i, cols, d):
                         acc = (acc1, acc3)[i]
-                        acc[i_e, :, cols] = d + jnp.where(k == 0, 0.0, acc[i_e, :, cols])
+                        acc[e, :, cols] = d + jnp.where(k == 0, 0.0, acc[e, :, cols])
 
                     two_products(
-                        abuf,
-                        xg[pl.ds(pl.multiple_of(i_e * CAP, CAP), CAP), :],
-                        lax.rem(kk * slots + i_e + EARLY, UP_SLOTS),
-                        put,
+                        abuf, xg[pl.ds(pl.multiple_of(e * CAP, CAP), CAP), :], lax.rem(q, UP_SLOTS), put
                     )
                 for u in range(2):
-                    start_up(kk * slots + g * 2 + u + EARLY + UP_SLOTS)
-
-                @pl.when((g == 1) & (kk + 1 < K_CHUNKS))
+                    start_up(k * experts + g * 2 + u + UP_SLOTS)
+                if last:
+                    for u in range(2):
+                        e = g * 2 + u
+                        inner[e] = (jax.nn.silu(acc1[e]) * acc3[e]).astype(BF16)
+                    return 0
+
+                @pl.when(g == 1)
                 def _():
-                    forward_far(kk + 1)
-
-                @pl.when((g == 0) & (kk + 2 < K_CHUNKS))
+                    forward_far(k + 1)
+
+                @pl.when((g == 1) & (k + 2 < K_CHUNKS))
                 def _():
-                    forward_near(kk + 2)
-
-                @pl.when(k == K_CHUNKS - 1)
-                def _():
-                    for u in range(2):
-                        i_e = g * 2 + u
-                        inner[base + i_e] = (jax.nn.silu(acc1[i_e]) * acc3[i_e]).astype(BF16)
+                    forward_near(k + 2)
 
                 return 0
 
             with jax.named_scope('up_steps'):
-                lax.fori_loop(0, slots // 2, up_step, 0)
-
+                lax.fori_loop(0, experts // 2, up_step, 0)
+
+        def up_chunk_step(k, _):
+            up_chunk(k, False)
             return 0
 
-        lax.fori_loop(0, 2 * K_CHUNKS, up_chunk, 0)
+        lax.fori_loop(0, K_CHUNKS - 1, up_chunk_step, 0)
+        up_chunk(jnp.int32(K_CHUNKS - 1), True)
         for i in range(1, n):
             info_copy(i, me, lax.rem(me + i, n)).wait_send()
         for k in range(K_CHUNKS):
             for lane_i in range(7):
                 rows_copy(jnp.int32(k), me, lane_i, sib).wait_send()
 
-    def phase_two(ebuf, part, sbuf):
-        late_shared(0, sbuf)
+    def phase_two(ebuf, part, sacc1, sacc3, sinner, sh, obuf, sbuf):
+        def shared_product(s, buf, slot):
+            k, h = s // halves, lax.rem(s, halves)
+
+            def put(i, cols, d):
+                acc = (sacc1, sacc3)[i]
+                acc[h, :, cols] = d + jnp.where(k == 0, 0.0, acc[h, :, cols])
+
+            two_products(buf, x_all[k, block(me), :], slot, put)
+
+        def late_copies(i):
+            slot = lax.rem(i, LATE_SLOTS)
+            return [
+                pltpu.make_async_copy(src, sbuf.at[slot, m], s_sem.at[slot, m]) for m, src in enumerate(shared_src(i))
+            ]
+
+        def late_turn(t):
+            @pl.when(t + 1 < N_CHUNKS)
+            def _():
+                for i in range(turn):
+                    late_start((t + 1) * turn + i)
+
+            with jax.named_scope('late_shared'):
+                for i in range(turn):
+                    for copy in late_copies(t * turn + i):
+                        copy.wait()
+                for i in range(turn):
+                    shared_product(t * turn + i, sbuf, lax.rem(t * turn + i, LATE_SLOTS))
+
+        def late_start(i):
+            for copy in late_copies(i):
+                copy.start()
+
+        for i in range(turn):
+            late_start(jnp.int32(i))
+
         def sib_copy(j, c):
             return remote(
                 part.at[j, block(c * 2 + (1 - core))], from_sib.at[j, c], sib_send.at[j, c], sib_recv.at[j, c], sib
@@ -500,14 +490,9 @@
             lax.fori_loop(0, 2, near, 0)
             far_onward(t)
 
-            @pl.when(t + 1 < late)
+            @pl.when(t >= 1)
             def _():
-                late_shared(t + 1, sbuf)
-
-            with jax.named_scope('late_shared'):
-                for copy in late_copies(t, sbuf):
-                    copy.wait()
-                shared_product(EARLY + t, sbuf, t)
+                late_turn(t - 1)
 
             @pl.when(t >= 1)
             def _():
@@ -517,24 +502,25 @@
 
         lax.fori_loop(0, N_CHUNKS, down_range, 0)
         last = jnp.int32(N_CHUNKS - 1)
+        near_home(last)
+
+        def own_spread(t, _):
+            spread(t, chip)
+            return 0
+
+        lax.fori_loop(0, N_CHUNKS, own_spread, 0)
+        late_turn(last)
         for h in range(halves):
             sinner[h] = (jax.nn.silu(sacc1[h]) * sacc3[h]).astype(BF16)
-
         for half in range(2):
 
-            def own_chip(i, _):
+            def shared_range(i, _):
                 shared_down(i, half)
-                if half == 0:
-
-                    @pl.when(i == 0)
-                    def _():
-                        near_home(last)
-
-                spread(half * (N_CHUNKS // 2) + i, chip)
                 return 0
 
-            lax.fori_loop(0, N_CHUNKS // 2, own_chip, 0)
-        far_home(last)
+            lax.fori_loop(0, N_CHUNKS // 2, shared_range, 0)
+            if half == 0:
+                far_home(last)
 
         def own_sums(t, _):
             add_sib(t, chip)
@@ -567,17 +553,22 @@
 
     pl.run_scoped(
         phase_one,
-        pltpu.VMEM((experts // 2 * CAP, kd), BF16),
+        pltpu.VMEM((experts * CAP, kd), BF16),
         pltpu.VMEM((experts * CAP, total), BF16),
-        pltpu.VMEM((experts // 2, CAP, ff), F32),
-        pltpu.VMEM((experts // 2, CAP, ff), F32),
+        pltpu.VMEM((experts, CAP, ff), F32),
+        pltpu.VMEM((experts, CAP, ff), F32),
         pltpu.VMEM((UP_SLOTS, 2, kd, ff), BF16),
     )
     pl.run_scoped(
         phase_two,
         pltpu.VMEM((N_CHUNKS, experts, CAP, nd), BF16),
         pltpu.VMEM((J_CHUNKS, total, jd), F32),
-        pltpu.VMEM((late, 2, kd, ff), BF16),
+        pltpu.VMEM((halves, rows, ff), F32),
+        pltpu.VMEM((halves, rows, ff), F32),
+        pltpu.VMEM((halves, rows, ff), BF16),
+        pltpu.VMEM((J_CHUNKS, rows, jd), F32),
+        pltpu.VMEM((rows, width), BF16),
+        pltpu.VMEM((LATE_SLOTS, 2, kd, ff), BF16),
     )
 
 
@@ -606,16 +597,11 @@
         vmem((experts, total, CAP), BF16),
         vmem((experts, total, 128), F32),
         vmem((experts, CAP, ff), BF16),
-        vmem((halves, rows, ff), F32),
-        vmem((halves, rows, ff), F32),
-        vmem((halves, rows, ff), BF16),
-        vmem((J_CHUNKS, rows, jd), F32),
         vmem((J_CHUNKS, chips, rows, jd), F32),
         vmem((J_CHUNKS, rows, jd), F32),
         vmem((2, J_CHUNKS, rows, jd), F32),
         vmem((experts // 2, ff, nd), BF16),
         vmem((experts // 2, ff, nd), BF16),
-        vmem((rows, width), BF16),
         pltpu.SMEM((1, 1), jnp.int32),
         dma((4,)),
         dma((n,)),
@@ -623,7 +609,7 @@
         dma((K_CHUNKS, 7)),
         dma((K_CHUNKS, n)),
         dma((UP_SLOTS, 2)),
-        dma((K_CHUNKS * halves - EARLY, 2)),
+        dma((LATE_SLOTS, 2)),
         dma((experts,)),
         dma((J_CHUNKS, chips)),
         dma((J_CHUNKS, chips)),

time: 78.4 us -> 78.3 us (level)
  no operation moved by 1% of the time
where the time goes in v4:
time: 78.3 us; the launch traced here: 78.1 us
  Pallas kernels  75.6 us (97%)
  local copies, waits for them, and re-layouts  1.77 us (2%)
    pallas_call x1, Pallas kernels, routed_layer(): pl.pallas_call(functools.partial(moe_kernel, n), out_shape=[jax.ShapeDtyp...  75.6 us
    unnamed x1, local copies, waits for them, and re-layouts  1.77 us

profile of v4, /device:TPU:81, one launch (start us, length us, event | category | flops | bytes accessed | tf_op | source)
XLA Modules:
  0.0 78.1 jit_solution(14282143837741280660)
XLA Ops:
  0.0 75.6 %moe_layer.1 = (bf16[96,2048]{1,0:T(8,128)(2,1)}, s32[1,1]{1,0:T(1,128)}) custom-call(bf16[96,2048]{1,0:T(8,128)(2,1)} %hid_hbm.1, bf16[16,128]{1,0:T(8,128)(2,1)} %bitcast.81, bf16[64,2048]{1,0:T(8,128)(2,1)} %bitcast.78, bf16[2048,2816]{1,0:T(8,128)(2,1)} %w1s.1, bf16[2048,2816]{1,0:T(8,128)(2,1)} %w3s.1, bf16[2816,2048]{1,0:T(8,128)(2,1)} %w2s.1, ...), custom_call_target="tpu_custom_call" | custom-call | tf_op jit(solution)/shard_map/moe_layer/pallas_call | solution.py:624
  76.2 0.1 conditional.1
  76.4 1.8 %copy.40 = bf16[96,2048]{1,0:T(8,128)(2,1)} copy(bf16[96,2048]{1,0:T(8,128)(2,1)} %get-tuple-element.90) | data formatting | bytes 786432
